TPU v7x, 32 devices: a whole 2x2x4 slice. The times are simulated.
32 devices in a mesh: gx: 4 (over z), gy: 2 (over x), gz: 4 (over y, core).
Axes of the slice: x: 2, y: 2, z: 4, core: 2. Of those that a mesh axis runs over, the one named last changes fastest.
Arguments:
- fields_now: float32 [24, 32, 16, 512], P(None, 'gx', 'gy', 'gz'), may hold values from -6 to 6
- parent: float32 [24, 32, 16, 512], P(None, 'gx', 'gy', 'gz'), may hold values from -6 to 6
- advect: float32 [3, 24, 24], replicated, may hold values from -0.75 to 0.75
- diffuse: float32 [3, 24, 24], replicated, may hold values from -0.25 to 0.25
- box_shift: int32 [3], replicated, may hold values from 1 to 4
Outputs:
- section_slope: float32 [24, 32, 16, 512], P(None, 'gx', 'gy', 'gz')
- section_value: float32 [24, 32, 16, 512], P(None, 'gx', 'gy', 'gz')
All inputs are finite; a program needn't handle non-finite values.
Results may differ from a plain program's by a relative error of at most 0.0001.
Values sent between devices are 32-bit elements; how exact they have to be, the bound alone decides.
A program may use at most 64 MiB of HBM per device.

v0:
```python
import functools

import jax
import jax.numpy as jnp
from jax import lax
from jax.experimental import pallas as pl
from jax.experimental.pallas import tpu as pltpu
from jax.sharding import PartitionSpec as P

MESH = pl.DeviceIdType.MESH
W = 4
H = 3
SLOT = 8
ROWS = 8
AXES = ("gx", "gy", "gz")


def roll(value, by):
    return pltpu.roll(value, by % value.shape[-1], value.ndim - 1)


def kernel(
    dims, shift_hbm, now_hbm, parent_hbm, advect_hbm, diffuse_hbm, slope_ref, value_ref,
    shift_ref, now_ref, parent_ref, advect_ref, diffuse_ref, box, edge, edge_in, rim, rim_up, rim_low, mixed, smooth_ref,
    send_sem, recv_sem, load_sem, *old,
):
    F, NX, NY, NZ = dims
    chunks = F // ROWS
    cells = NX * NY
    slots = NZ // SLOT
    groups = cells // slots
    me = {a: lax.axis_index(a) for a in AXES}
    size = {a: lax.axis_size(a) for a in AXES}
    below = {a: me[a] > 0 for a in AXES}
    above = {a: me[a] < size[a] - 1 for a in AXES}
    sems = iter(range(11 * chunks))

    loads = []
    span = ROWS * cells
    for c in range(chunks):
        part = pl.ds(c * span, span)
        loads.append(pltpu.make_async_copy(now_hbm.at[part], now_ref.at[part], load_sem.at[c]))
    loads += [
        pltpu.make_async_copy(src, dst, load_sem.at[chunks + n])
        for n, (src, dst) in enumerate((
            (shift_hbm, shift_ref), (parent_hbm, parent_ref),
            (advect_hbm, advect_ref), (diffuse_hbm, diffuse_ref),
        ))
    ]
    for n in (0, chunks, *range(1, chunks), *range(chunks + 1, chunks + 4)):
        loads[n].start()

    class Copy:
        def __init__(self, src, dst, axis, by):
            n = next(sems)
            self.sends = below[axis] if by < 0 else above[axis]
            self.gets = above[axis] if by < 0 else below[axis]
            self.copy = pltpu.make_async_remote_copy(
                src_ref=src, dst_ref=dst, send_sem=send_sem.at[n], recv_sem=recv_sem.at[n],
                device_id={axis: me[axis] + by}, device_id_type=MESH,
            )

        def start(self):
            pl.when(self.sends)(self.copy.start)

        def arrived(self):
            pl.when(self.gets)(self.copy.wait_recv)

        def sent(self):
            pl.when(self.sends)(self.copy.wait_send)

    rim_up[...] = jnp.zeros_like(rim_up)
    rim_low[...] = jnp.zeros_like(rim_low)
    blank = jnp.zeros((ROWS, NZ), jnp.float32)

    def clear_x(y, _):
        for c in range(chunks):
            for x in (*range(H), *range(NX + H, NX + 2 * H)):
                box[c, x, y + H] = blank
        return 0

    def clear_y(x, _):
        for c in range(chunks):
            for y in (*range(H), *range(NY + H, NY + 2 * H)):
                box[c, x + H, y] = blank
        return 0

    lax.fori_loop(0, NY, clear_x, 0)
    lax.fori_loop(0, NX, clear_y, 0)

    barrier = pltpu.get_barrier_semaphore()
    count = 0
    for a in AXES:
        for cond, by in ((below[a], -1), (above[a], 1)):
            @pl.when(cond)
            def _(a=a, by=by):
                pl.semaphore_signal(
                    barrier, inc=1, device_id={a: me[a] + by}, device_id_type=MESH
                )
        count = count + jnp.where(me[a] > 0, 1, 0) + jnp.where(me[a] < size[a] - 1, 1, 0)

    lane = lax.broadcasted_iota(jnp.int32, (ROWS, NZ), 1)
    slot_of = ((lane + SLOT // 2) % NZ) // SLOT

    def place(g, j):
        k = g * slots + j
        return k, g * (slots // NY) + j // NY, j % NY

    def rows_of(c, k):
        return pl.ds(c * ROWS * cells + k, ROWS, stride=cells)

    def pack_old(c):
        def step(g, _):
            packed = blank
            for j in range(slots):
                k, _, _ = place(g, j)
                packed = jnp.where(slot_of == j, roll(now_ref[rows_of(c, k), :], SLOT * j), packed)
            edge[c, g] = packed
            return 0

        lax.fori_loop(0, groups, step, 0)

    edges = [Copy(edge.at[c], edge_in.at[c], "gz", -1) for c in range(chunks)]
    for c in range(chunks):
        loads[c].wait()
        pack_old(c)
        if c == 0:
            pl.semaphore_wait(barrier, count)
        edges[c].start()

    X, Y = pl.ds(0, NX), pl.ds(0, NY)
    BX, BY = pl.ds(H, NX), pl.ds(H, NY)
    half = W // 2
    near, far = pl.ds(NX, half), pl.ds(NX + half, half)
    to_x, to_y, corner_y, corner_x, halos = [], [], [], [], []
    for c in range(chunks):
        o, b = old[c], box.at[c]
        to_x.append(Copy(o.at[pl.ds(0, W), Y], o.at[pl.ds(NX, W), Y], "gx", -1))
        to_y.append(Copy(o.at[X, pl.ds(0, W)], o.at[X, pl.ds(NY, W)], "gy", -1))
        corner_y.append(Copy(o.at[near, pl.ds(0, W)], o.at[near, pl.ds(NY, W)], "gy", -1))
        corner_x.append(
            Copy(o.at[pl.ds(half, half), pl.ds(NY, W)], o.at[far, pl.ds(NY, W)], "gx", -1)
        )
        halos.append([
            Copy(b.at[pl.ds(H, H), BY], b.at[pl.ds(NX + H, H), BY], "gx", -1),
            Copy(b.at[pl.ds(NX, H), BY], b.at[pl.ds(0, H), BY], "gx", 1),
            Copy(b.at[BX, pl.ds(H, H)], b.at[BX, pl.ds(NY + H, H)], "gy", -1),
            Copy(b.at[BX, pl.ds(NY, H)], b.at[BX, pl.ds(0, H)], "gy", 1),
            Copy(rim.at[c], rim_up.at[c], "gz", -1),
            Copy(rim.at[c], rim_low.at[c], "gz", 1),
        ])

    loads[chunks].wait()
    move = [shift_ref[d] for d in range(3)]

    def move_z(c):
        edges[c].arrived()

        def step(g, _):
            for j in range(slots):
                k, x, y = place(g, j)
                tail = roll(edge_in[c, g], -SLOT * j)
                row = jnp.where(lane < move[2], tail, now_ref[rows_of(c, k), :])
                old[c][x, y] = pltpu.roll(row, NZ - move[2], 1)
            return 0

        lax.fori_loop(0, groups, step, 0)

    def send_old(c):
        to_x[c].start()
        to_y[c].start()

    def send_corner(c):
        to_x[c].arrived()
        corner_y[c].start()
        to_y[c].arrived()
        corner_x[c].start()

    def send_halos(c, down):
        for n, h in enumerate(halos[c]):
            if (n in (0, 2)) == down:
                h.start()

    in_z = me["gz"] * NZ + lane + move[2] < size["gz"] * NZ

    def move_xy(c):
        corner_y[c].arrived()
        corner_x[c].arrived()

        def step(g, _):
            packed = blank
            for j in range(slots):
                k, x, y = place(g, j)
                in_x = me["gx"] * NX + x + move[0] < size["gx"] * NX
                in_y = me["gy"] * NY + y + move[1] < size["gy"] * NY
                row = jnp.where(
                    in_z & (in_x & in_y),
                    old[c][x + move[0], y + move[1]],
                    parent_ref[rows_of(c, k), :],
                )
                box[c, x + H, y + H] = row
                packed = jnp.where(slot_of == j, roll(row, SLOT * j), packed)
            rim[c, g] = packed
            return 0

        lax.fori_loop(0, groups, step, 0)
        send_halos(c, False)

    def split(value):
        high = value.astype(jnp.bfloat16)
        return high, (value - high.astype(jnp.float32)).astype(jnp.bfloat16)

    def terms(u, at):
        d1, s1 = at(1) - at(-1), at(1) + at(-1)
        d2, s2 = at(2) - at(-2), at(2) + at(-2)
        s3 = at(3) + at(-3)
        first = 8.0 * d1 - d2
        second = 16.0 * s1 - 30.0 * u - s2
        sixth = s3 - 6.0 * s2 + 15.0 * s1 - 20.0 * u
        return first, second, sixth

    def compute(c):
        for h in halos[c]:
            h.arrived()
        fields = slice(c * ROWS, (c + 1) * ROWS)
        mats = [m[a][:, fields] for a in range(3) for m in (advect_ref, diffuse_ref)]
        m_high, m_low = split(jnp.concatenate(mats, axis=1) / 12.0)
        dot = functools.partial(jnp.dot, preferred_element_type=jnp.float32)

        def step(g, _):
            rims = jnp.where(lane % SLOT < SLOT // 2, rim_up[c, g], rim_low[c, g])
            for j0 in range(0, slots, 2):
                columns = []
                for j in (j0, j0 + 1):
                    k, x, y = place(g, j)
                    u = box[c, x + H, y + H]
                    ends = roll(rims, -SLOT * j)
                    z_at = {}
                    for o in range(1, H + 1):
                        z_at[o] = roll(jnp.where(lane < o, ends, u), -o)
                        z_at[-o] = roll(jnp.where(lane >= NZ - o, ends, u), o)
                    fx, sx, x6 = terms(u, lambda o: box[c, x + H + o, y + H])
                    fy, sy, y6 = terms(u, lambda o: box[c, x + H, y + H + o])
                    fz, sz, z6 = terms(u, lambda o: z_at[o])
                    columns.append(jnp.concatenate([fx, sx, fy, sy, fz, sz], axis=0))
                    smooth_ref[c, k] = (x6 + y6 + z6) * (1.0 / 64.0)
                high, low = split(jnp.concatenate(columns, axis=1))
                linear = dot(m_high, high) + (dot(m_low, high) + dot(m_high, low))
                for i in range(2):
                    k = g * slots + j0 + i
                    part = linear[:, i * NZ:(i + 1) * NZ]
                    if c > 0:
                        part = part + mixed[k]
                    if c < chunks - 1:
                        mixed[k] = part
                        continue
                    _, x, y = place(g, j0 + i)
                    lapse = 1.0 + 0.25 * jnp.tanh(box[0, x + H, y + H][0:1, :])
                    for n in range(chunks):
                        slope = lapse * part[n * ROWS:(n + 1) * ROWS] + smooth_ref[n, k]
                        slope_ref[rows_of(n, k), :] = slope
                        value_ref[rows_of(n, k), :] = box[n, x + H, y + H] + 0.125 * slope
            return 0

        lax.fori_loop(0, groups, step, 0)

    move_z(0)
    send_old(0)
    for c in range(1, chunks):
        move_z(c)
    for load in loads[chunks + 1:]:
        load.wait()
    for c in range(chunks):
        to_x[c].sent()
        to_y[c].sent()
        if c + 1 < chunks:
            send_old(c + 1)
            send_corner(c)
        if c > 0:
            move_xy(c - 1)
            if c + 1 == chunks:
                for n in range(c):
                    send_halos(n, True)
    last = chunks - 1
    send_corner(last)
    move_xy(last)
    send_halos(last, True)
    for c in range(chunks):
        compute(c)

    for c in range(chunks):
        edges[c].sent()
    for c in range(chunks):
        corner_y[c].sent()
        corner_x[c].sent()
        for h in halos[c]:
            h.sent()


def local(fields_now, parent, advect, diffuse, box_shift):
    dims = fields_now.shape
    F, NX, NY, NZ = dims
    flat = (F * NX * NY, NZ)
    chunks = F // ROWS
    groups = NX * NY * SLOT // NZ
    f32 = jnp.float32
    edges = pltpu.VMEM((chunks, groups, ROWS, NZ), f32)
    vmem = pl.BlockSpec(memory_space=pltpu.VMEM)
    slope, value = pl.pallas_call(
        functools.partial(kernel, dims),
        out_shape=[jax.ShapeDtypeStruct(flat, f32)] * 2,
        in_specs=[pl.BlockSpec(memory_space=pltpu.HBM)] * 5,
        out_specs=[vmem] * 2,
        scratch_shapes=[
            pltpu.SMEM(box_shift.shape, jnp.int32),
            pltpu.VMEM(flat, f32),
            pltpu.VMEM(flat, f32),
            pltpu.VMEM(advect.shape, f32),
            pltpu.VMEM(diffuse.shape, f32),
            pltpu.VMEM((chunks, NX + 2 * H, NY + 2 * H, ROWS, NZ), f32),
            edges, edges, edges, edges, edges,
            pltpu.VMEM((NX * NY, F, NZ), f32),
            pltpu.VMEM((chunks, NX * NY, ROWS, NZ), f32),
            pltpu.SemaphoreType.DMA((11 * chunks,)),
            pltpu.SemaphoreType.DMA((11 * chunks,)),
            pltpu.SemaphoreType.DMA((chunks + 4,)),
        ] + [pltpu.VMEM((NX + W, NY + W, ROWS, NZ), f32)] * chunks,
        compiler_params=pltpu.CompilerParams(
            collective_id=0, has_side_effects=True
        ),
    )(box_shift, fields_now.reshape(flat), parent.reshape(flat), advect, diffuse)
    return slope.reshape(dims), value.reshape(dims)


def solution(mesh):
    return jax.shard_map(
        local,
        mesh=mesh,
        in_specs=(P(None, "gx", "gy", "gz"), P(None, "gx", "gy", "gz"), P(), P(), P()),
        out_specs=(P(None, "gx", "gy", "gz"), P(None, "gx", "gy", "gz")),
        check_vma=False,
    )
```

profile of v0, /device:TPU:0, one launch (start us, length us, event | category | flops | bytes accessed | tf_op | source)
XLA Modules:
  0.0 38.2 jit_solution(5892753887358299218)
XLA Ops:
  0.6 34.5 %shard_map.68 = (f32[1536,128]{1,0:T(8,128)}, f32[1536,128]{1,0:T(8,128)}) custom-call(s32[3]{0:T(128)} %shift_hbm.1, f32[1536,128]{1,0:T(8,128)} %bitcast.4, f32[1536,128]{1,0:T(8,128)} %bitcast.5, f32[3,24,24]{2,1,0:T(8,128)} %advect_hbm.1, f32[3,24,24]{2,1,0:T(8,128)} %diffuse_hbm.1), custom_call_target="tpu_custom_call" | custom-call | tf_op jit(solution)/shard_map/pallas_call | solution.py:309
  35.1 0.0 copy-start
  35.1 2.2 %copy.9 = f32[24,8,8,128]{3,2,1,0:T(8,128)} copy(f32[24,8,8,128]{3,2,1,0:T(8,128)} %bitcast.7) | data formatting | bytes 1572864
  37.3 0.0 copy-done
  37.3 0.9 %copy.10 = f32[24,8,8,128]{3,2,1,0:T(8,128)} copy(f32[24,8,8,128]{3,2,1,0:T(8,128)S(1)} %bitcast.6) | data formatting | bytes 1572864
Async XLA Ops:
  35.1 2.2 %copy-start = (f32[1536,128]{1,0:T(8,128)S(1)}, f32[1536,128]{1,0:T(8,128)}, u32[]{:S(2)}) copy-start(f32[1536,128]{1,0:T(8,128)} %get-tuple-element.5) | copy-start | bytes 2359300
where the time goes:
time: 38.3 us; the launch traced here: 38.2 us
  Pallas kernels  34.5 us (90%)
  local copies, waits for them, and re-layouts  3.04 us (8%)
  between operations  0.65 us (2%)
    pallas_call x1, Pallas kernels, local(): pl.pallas_call(functools.partial(kernel, dims), out_shape=[jax.ShapeDtype...  34.5 us
    unnamed x4, local copies, waits for them, and re-layouts  3.04 us

commit v1 on v0

v1 whole, which is shorter than its diff:
```python
import functools

import jax
import jax.numpy as jnp
import numpy as np
from jax import lax
from jax.experimental import pallas as pl
from jax.experimental.pallas import tpu as pltpu
from jax.sharding import PartitionSpec as P

MESH = pl.DeviceIdType.MESH
W = 4
H = 3
SLOT = 8
ROWS = 8
AXES = ("gx", "gy", "gz")
KINDS = ("x", "y", "xy")
MESSAGES = {"x": 12, "y": 12, "xy": 15}
FIRST = {-2: 1, -1: -8, 1: 8, 2: -1}
SECOND = {-2: -1, -1: 16, 0: -30, 1: 16, 2: -1}
SIXTH = {-3: 1, -2: -6, -1: 15, 0: -20, 1: 15, 2: -6, 3: 1}
BLOCKS = [(None, 0)] + [(a, o) for a in range(3) for o in (-3, -2, -1, 1, 2, 3)]
SIDES = [(a, sign) for a in range(2) for sign in (-1, 1)]
f32, bf16 = jnp.float32, jnp.bfloat16


def up_to(n, m):
    return -(-n // m) * m


def block_columns(block, fields):
    cols = np.zeros((16, 2 * fields), np.float32)
    for c in range(fields // ROWS):
        for h in range(2):
            for r in range(ROWS):
                n = (c * 2 + h) * ROWS + r
                cols[7, n] = c * ROWS + r
                cols[8, n] = 1 - h
    if block is None:
        return cols
    axis, o = block
    for a in range(3):
        if axis is None or a == axis:
            cols[a] = FIRST.get(o, 0)
            cols[3 + a] = SECOND.get(o, 0)
            cols[6] += SIXTH[o]
    return cols


def coefficients(fields):
    groups = [BLOCKS]
    for a, sign in SIDES:
        near = [(a, sign * o) for o in range(1, H + 1)]
        groups += [near[d:] + [None] * d for d in range(H)]
    out = []
    for g in groups:
        cols = np.concatenate([block_columns(b, fields) for b in g], axis=1)
        out.append(np.pad(cols, ((0, 0), (0, up_to(cols.shape[1], 256) - cols.shape[1]))))
    return np.concatenate(out, axis=1)


def scratch(dims):
    F, NX, NY, NZ = dims
    chunks = F // ROWS
    groups = NX * NY * SLOT // NZ
    tile = (ROWS, NZ)
    out = dict(
        shift=pltpu.SMEM((3,), jnp.int32),
        own=pltpu.VMEM((NX, NY, F, NZ), f32),
        par=pltpu.VMEM((NX, NY, F, NZ), f32),
        advect=pltpu.VMEM((3, F, F), f32),
        diffuse=pltpu.VMEM((3, F, F), f32),
        coef=pltpu.VMEM(coefficients(F).shape, f32),
        w_early=pltpu.VMEM((3 * F, len(BLOCKS) * 2 * F), bf16),
        w_late=pltpu.VMEM((len(SIDES), 7 * F, H * 2 * F), bf16),
        box=pltpu.VMEM((NX + 2 * H, NY + 2 * H, F, NZ), f32),
        ub=pltpu.VMEM((NX + 2 * H, NY + 2 * H, chunks, 2 * ROWS, NZ), bf16),
        acc=pltpu.VMEM((NX, NY, 2 * F, NZ), f32),
        rim=pltpu.VMEM((chunks, groups) + tile, f32),
        rim_up=pltpu.VMEM((chunks, groups) + tile, f32),
        rim_low=pltpu.VMEM((chunks, groups) + tile, f32),
        epk=pltpu.VMEM((chunks, 3) + tile, f32),
        ein=pltpu.VMEM((chunks, 4) + tile, f32),
    )
    for c in range(chunks):
        kind = KINDS[c % 3]
        if "x" in kind:
            out[f"rawx{c}"] = pltpu.VMEM((W, NY) + tile, f32)
        if "y" in kind:
            out[f"rawy{c}"] = pltpu.VMEM((NX, W) + tile, f32)
        ext = (W if "x" in kind else 0, W if "y" in kind else 0)
        out[f"zs{c}"] = pltpu.VMEM((NX + ext[0], NY + ext[1]) + tile, f32)
        if kind == "xy":
            out[f"ce{c}"] = pltpu.VMEM((W, W) + tile, f32)
        else:
            size = (NX, W) if kind == "x" else (W, NY)
            out[f"fw{c}"] = pltpu.VMEM(size + tile, f32)
            out[f"te{c}"] = pltpu.VMEM(size + tile, f32)
    n = sum(MESSAGES[KINDS[c % 3]] for c in range(chunks))
    out["send_sem"] = pltpu.SemaphoreType.DMA((n,))
    out["recv_sem"] = pltpu.SemaphoreType.DMA((n,))
    out["load_sem"] = pltpu.SemaphoreType.DMA((6,))
    return out


def kernel(
    dims, shift_hbm, now_hbm, parent_hbm, advect_hbm, diffuse_hbm, coef_hbm, slope_ref, value_ref, *refs
):
    F, NX, NY, NZ = dims
    chunks = F // ROWS
    cells = NX * NY
    s = dict(zip(scratch(dims), refs))
    own, par, box, ub, acc = s["own"], s["par"], s["box"], s["ub"], s["acc"]
    epk, ein, rim, rim_up, rim_low = s["epk"], s["ein"], s["rim"], s["rim_up"], s["rim_low"]
    slots = NZ // SLOT
    groups = cells // slots
    me = {a: lax.axis_index(a) for a in AXES}
    size = {a: lax.axis_size(a) for a in AXES}
    below = {a: me[a] > 0 for a in AXES}
    above = {a: me[a] < size[a] - 1 for a in AXES}
    sems = iter(range(1000))
    kinds = [KINDS[c % 3] for c in range(chunks)]
    rows = [pl.ds(c * ROWS, ROWS) for c in range(chunks)]

    def load_cell(src, dst, n, k):
        return pltpu.make_async_copy(src.at[:, k], dst.at[k // NY, k % NY], s["load_sem"].at[n])

    def load_cells(src, dst, n):
        def step(k, _):
            load_cell(src, dst, n, k).start()
            return 0

        lax.fori_loop(0, cells, step, 0, unroll=8)

    singles = [
        pltpu.make_async_copy(src, dst, s["load_sem"].at[2 + n])
        for n, (src, dst) in enumerate((
            (shift_hbm, s["shift"]), (advect_hbm, s["advect"]),
            (diffuse_hbm, s["diffuse"]), (coef_hbm, s["coef"]),
        ))
    ]
    singles[0].start()
    load_cells(now_hbm, own, 0)

    class Copy:
        def __init__(self, src, dst, to, parts=None):
            n = next(sems)
            self.to = to
            self.sem = dict(send_sem=s["send_sem"].at[n], recv_sem=s["recv_sem"].at[n])
            self.parts = parts
            self.copy = self.make(src, dst)
            self.sends = self.gets = None
            for a, by in to.items():
                sends = below[a] if by < 0 else above[a]
                gets = above[a] if by < 0 else below[a]
                self.sends = sends if self.sends is None else self.sends & sends
                self.gets = gets if self.gets is None else self.gets & gets

        def make(self, src, dst):
            return pltpu.make_async_remote_copy(
                src_ref=src, dst_ref=dst, device_id={a: me[a] + by for a, by in self.to.items()},
                device_id_type=MESH, **self.sem,
            )

        def start(self):
            pl.when(self.sends)(self.copy.start)

        def start_part(self, i):
            pl.when(self.sends)(self.make(*self.parts(i)).start)

        def arrived(self):
            pl.when(self.gets)(self.copy.wait_recv)

        def sent(self):
            pl.when(self.sends)(self.copy.wait_send)

    everything = []

    def message(src, dst, to, parts=None):
        everything.append(Copy(src, dst, to, parts))
        return everything[-1]

    DX, DY, DZ = {"gx": -1}, {"gy": -1}, {"gz": -1}
    UX, UY, UZ = {"gx": 1}, {"gy": 1}, {"gz": 1}
    lowx, lowy = pl.ds(0, W), pl.ds(0, W)
    raw, edge, diag, forward, corner = {}, {}, {}, {}, {}
    for c, kind in enumerate(kinds):
        if kind == "x":
            def cell(i, half, c=c):
                x, y = i // W, i % W + half * (NY // 2)
                return now_hbm.at[rows[c], x * NY + y], s[f"rawx{c}"].at[x, y]

            halves = [s[f"rawx{c}"].at[:, pl.ds(h * (NY // 2), NY // 2)] for h in range(2)]
            raw[c] = [message(r, r, DX, functools.partial(cell, half=h)) for h, r in enumerate(halves)]
            diag[c] = [message(epk.at[c, 0], ein.at[c, 2], DX | DZ)]
            forward[c] = message(s[f"fw{c}"], s[f"te{c}"], DY)
        elif kind == "y":
            def cell(i, half, c=c):
                x, y = i // W + half * (NX // 2), i % W
                return now_hbm.at[rows[c], x * NY + y], s[f"rawy{c}"].at[x, y]

            halves = [s[f"rawy{c}"].at[pl.ds(h * (NX // 2), NX // 2)] for h in range(2)]
            raw[c] = [message(r, r, DY, functools.partial(cell, half=h)) for h, r in enumerate(halves)]
            diag[c] = [message(epk.at[c, 0], ein.at[c, 2], DY | DZ)]
            forward[c] = message(s[f"fw{c}"], s[f"te{c}"], DX)
        else:
            raw[c] = [
                message(own.at[lowx, :, rows[c]], s[f"rawx{c}"], DX),
                message(own.at[:, lowy, rows[c]], s[f"rawy{c}"], DY),
            ]
            diag[c] = [
                message(epk.at[c, 0], ein.at[c, 2], DX | DZ), message(epk.at[c, 2], ein.at[c, 3], DY | DZ),
            ]
            near, far = pl.ds(0, W // 2), pl.ds(W // 2, W // 2)
            zs, ce = s[f"zs{c}"], s[f"ce{c}"]
            corner[c] = [
                message(zs.at[far, pl.ds(NY, W)], ce.at[far], DX),
                message(zs.at[pl.ds(NX, W // 2), lowy], ce.at[near], DY),
            ]
        edge[c] = message(epk.at[c, pl.ds(0, 2)], ein.at[c, pl.ds(0, 2)], DZ)

    inside = {side: [] for side in SIDES}

    def halo(c, a, by, lo, hi):
        n = (NX, NY)[a]
        src = pl.ds(H, H) if by < 0 else pl.ds(n, H)
        dst = pl.ds(n + H, H) if by < 0 else pl.ds(0, H)
        span = pl.ds(H + lo, hi - lo)
        to = {AXES[a]: by}
        if a == 0:
            m = message(box.at[src, span, rows[c]], box.at[dst, span, rows[c]], to)
        else:
            m = message(box.at[span, src, rows[c]], box.at[span, dst, rows[c]], to)
        inside[(a, -by)].append(m)
        return m

    early_halo, late_halo, rims = {}, {}, {}
    hx, hy = NX // 2, NY // 2
    for c, kind in enumerate(kinds):
        if kind == "x":
            early_halo[c] = [halo(c, 1, -1, 0, NX), halo(c, 0, 1, 0, hy)]
            late_halo[c] = [halo(c, 0, -1, 0, NY), halo(c, 0, 1, hy, NY), halo(c, 1, 1, 0, NX)]
        elif kind == "y":
            early_halo[c] = [halo(c, 0, -1, 0, NY), halo(c, 1, 1, 0, hx)]
            late_halo[c] = [halo(c, 1, -1, 0, NX), halo(c, 1, 1, hx, NX), halo(c, 0, 1, 0, NY)]
        else:
            early_halo[c] = [halo(c, 0, -1, 0, NY), halo(c, 1, -1, 0, NX), halo(c, 0, 1, 0, hy), halo(c, 1, 1, 0, hx)]
            late_halo[c] = [halo(c, 0, 1, hy, NY), halo(c, 1, 1, hx, NX)]
        rims[c] = [message(rim.at[c], rim_up.at[c], DZ), message(rim.at[c], rim_low.at[c], UZ)]

    barrier = pltpu.get_barrier_semaphore()
    count = 0
    for to in (DX, UX, DY, UY, DZ, UZ, UX | UZ, UY | UZ):
        cond = back = None
        for a, by in to.items():
            one, two = (below[a], above[a]) if by < 0 else (above[a], below[a])
            cond = one if cond is None else cond & one
            back = two if back is None else back & two

        @pl.when(cond)
        def _(to=to):
            pl.semaphore_signal(
                barrier, inc=1, device_id={a: me[a] + by for a, by in to.items()}, device_id_type=MESH
            )
        count = count + jnp.where(back, 1, 0)

    load_cells(parent_hbm, par, 1)
    for load in singles[1:]:
        load.start()
    pl.semaphore_wait(barrier, count)

    def send_raw(i, _, half):
        for c, kind in enumerate(kinds):
            if kind != "xy":
                raw[c][half].start_part(i)
        return 0

    for half in range(2):
        lax.fori_loop(0, W * W, functools.partial(send_raw, half=half), 0, unroll=4)

    lane = lax.broadcasted_iota(jnp.int32, (ROWS, NZ), 1)
    thin = lane // W
    wide = ((lane + SLOT // 2) % NZ) // SLOT
    blank = jnp.zeros((ROWS, NZ), f32)

    def pack(c, n, along, q):
        def step(i, packed):
            for j in range(NY if along == "x" else NX):
                x, y = (q * W + i, j) if along == "x" else (j, q * W + i)
                slot = i * (NY if along == "x" else NX) + j
                packed = jnp.where(thin == slot, pltpu.roll(own[x, y, rows[c]], W * slot, 1), packed)
            return packed

        epk[c, n] = lax.fori_loop(0, W, step, blank)

    pltpu.make_async_copy(par, own, s["load_sem"].at[0]).wait()
    for c, kind in enumerate(kinds):
        along = kind[0]
        for q in range(2):
            pack(c, q, along, q)
        if kind == "xy":
            pack(c, 2, "y", 0)
        for d in diag[c]:
            d.start()
        edge[c].start()
    for c, kind in enumerate(kinds):
        if kind == "xy":
            for r in raw[c]:
                r.start()

    zero16 = jnp.zeros((2 * ROWS, NZ), bf16)

    def clear(i, _):
        for o in (*range(H), *range(H)):
            pass
        for c in range(chunks):
            for o in range(H):
                ub[o, i + H, c] = zero16
                ub[NX + H + o, i + H, c] = zero16
                ub[i + H, o, c] = zero16
                ub[i + H, NY + H + o, c] = zero16
        return 0

    lax.fori_loop(0, NX, clear, 0)

    for load in singles:
        load.wait()
    move = [s["shift"][d] for d in range(3)]
    sz = move[2]

    def split16(u):
        low = u - u.astype(bf16).astype(f32)
        return jnp.concatenate([u, low], axis=0).astype(bf16)

    def weights():
        mats = []
        for m in (s["advect"], s["diffuse"]):
            for a in range(3):
                one = m[a]
                high = one.astype(bf16).astype(f32)
                mid = (one - high).astype(bf16).astype(f32)
                mats.append(jnp.concatenate([high, mid, one - high - mid], axis=0).astype(bf16))

        def columns(at, width, ks):
            table = s["coef"][:, at:at + width]
            hit = lax.broadcasted_iota(jnp.int32, (F, width), 0).astype(f32) == table[7:8]
            smooth = jnp.where(hit, table[6:7], 0.0)
            if not ks:
                return smooth
            total = None
            for k in ks:
                spread = jnp.where(hit, table[k:k + 1], 0.0).astype(bf16)
                part = jnp.dot(mats[k], spread, preferred_element_type=f32)
                total = part if total is None else total + part
            w = total[:F] + total[F:2 * F] + total[2 * F:]
            high = w.astype(bf16).astype(f32)
            return jnp.concatenate([high, (w - high) * table[8:9], smooth], axis=0)

        k_early = len(BLOCKS) * 2 * F
        for at in range(0, up_to(k_early, 256), 256):
            n = min(256, k_early - at)
            s["w_early"][:, at:at + n] = columns(at, 256, range(6))[:, :n].astype(bf16)
        at = up_to(k_early, 256)
        k_late = H * 2 * F
        step = up_to(k_late, 256)
        for n, (a, sign) in enumerate(SIDES):
            parts = [columns(at + d * step, step, (a, 3 + a) if d < 2 else ()) for d in range(H)]
            s["w_late"][n] = jnp.concatenate(parts, axis=0)[:, :k_late].astype(bf16)
            at += H * step

    weights()

    def z_row(row, packed, slot):
        tail = pltpu.roll(packed, lax.rem(2 * NZ - W * slot - sz, NZ), 1)
        return jnp.where(lane >= NZ - sz, tail, pltpu.roll(row, NZ - sz, 1))

    def z_own(c):
        kind = kinds[c]

        def step(x, _):
            for y in range(NY):
                q, slot = (x // W, x % W * NY + y) if "x" in kind else (y // W, y % W * NX + x)
                s[f"zs{c}"][x, y] = z_row(own[x, y, rows[c]], ein[c, q], slot)
            return 0

        lax.fori_loop(0, NX, step, 0)

    def z_ext_x(c, lo, hi):
        def step(x, _):
            for y in range(lo, hi):
                s[f"zs{c}"][NX + x, y] = z_row(s[f"rawx{c}"][x, y], ein[c, 2], x * NY + y)
            return 0

        lax.fori_loop(0, W, step, 0)

    def z_ext_y(c, lo, hi):
        n = 3 if kinds[c] == "xy" else 2

        def step(x, _):
            for y in range(W):
                s[f"zs{c}"][x, NY + y] = z_row(s[f"rawy{c}"][x, y], ein[c, n], y * NX + x)
            return 0

        lax.fori_loop(lo, hi, step, 0)

    def make_forward(c):
        zs, fw = s[f"zs{c}"], s[f"fw{c}"]

        def step(i, _):
            for j in range(W):
                if kinds[c] == "x":
                    fw[i, j] = zs[i + move[0], j]
                else:
                    fw[j, i] = zs[j, i + move[1]]
            return 0

        lax.fori_loop(0, NX if kinds[c] == "x" else NY, step, 0)

    in_z = me["gz"] * NZ + lane + sz < size["gz"] * NZ

    def renew(c, xs, ys, late):
        kind, zs = kinds[c], s[f"zs{c}"]

        def step(x, _):
            in_x = me["gx"] * NX + x + move[0] < size["gx"] * NX
            for y in range(*ys):
                in_y = me["gy"] * NY + y + move[1] < size["gy"] * NY
                X, Y = x + move[0], y + move[1]
                if not late:
                    row = zs[X, Y]
                elif kind == "x":
                    row = jnp.where(Y < NY, zs[X, jnp.minimum(Y, NY - 1)], s[f"te{c}"][x, jnp.maximum(Y - NY, 0)])
                elif kind == "y":
                    row = jnp.where(X < NX, zs[jnp.minimum(X, NX - 1), Y], s[f"te{c}"][jnp.maximum(X - NX, 0), y])
                else:
                    row = jnp.where(
                        (X < NX) | (Y < NY), zs[X, Y],
                        s[f"ce{c}"][jnp.maximum(X - NX, 0), jnp.maximum(Y - NY, 0)],
                    )
                row = jnp.where(in_z & (in_x & in_y), row, par[x, y, rows[c]])
                box[x + H, y + H, rows[c]] = row
                ub[x + H, y + H, c] = split16(row)
            return 0

        lax.fori_loop(*xs, step, 0)

    def renew_early(c):
        if kinds[c] == "x":
            renew(c, (0, NX), (0, hy), False)
        elif kinds[c] == "y":
            renew(c, (0, hx), (0, NY), False)
        else:
            renew(c, (0, hx), (0, NY), False)
            renew(c, (hx, NX), (0, hy), False)
        for h in early_halo[c]:
            h.start()

    def renew_late(c):
        if kinds[c] == "x":
            renew(c, (0, NX), (hy, NY), True)
        elif kinds[c] == "y":
            renew(c, (hx, NX), (0, NY), True)
        else:
            renew(c, (hx, NX), (hy, NY), True)
        for h in late_halo[c]:
            h.start()

        def step(g, _):
            packed = blank
            for j in range(slots):
                x, y = g * (slots // NY) + j // NY, j % NY
                packed = jnp.where(wide == j, pltpu.roll(box[x + H, y + H, rows[c]], SLOT * j, 1), packed)
            rim[c, g] = packed
            return 0

        lax.fori_loop(0, groups, step, 0)
        for r in rims[c]:
            r.start()

    one_way = [c for c in range(chunks) if kinds[c] != "xy"]
    both = [c for c in range(chunks) if kinds[c] == "xy"]
    for c in one_way:
        edge[c].arrived()
        z_own(c)
    for c in one_way:
        diag[c][0].arrived()
        raw[c][0].arrived()
        if kinds[c] == "x":
            z_ext_x(c, 0, hy)
        else:
            z_ext_y(c, 0, hx)
        make_forward(c)
        forward[c].start()
    for c in both:
        edge[c].arrived()
        z_own(c)
    for c in one_way:
        raw[c][1].arrived()
        if kinds[c] == "x":
            z_ext_x(c, hy, NY)
        else:
            z_ext_y(c, hx, NX)
    for c in both:
        for d in diag[c]:
            d.arrived()
        raw[c][0].arrived()
        z_ext_x(c, 0, NY)
        raw[c][1].arrived()
        z_ext_y(c, 0, NX)
        for k in corner[c]:
            k.start()
    pltpu.make_async_copy(own, par, s["load_sem"].at[1]).wait()
    for c in (*one_way, *both):
        renew_early(c)
    for c in one_way:
        forward[c].arrived()
        renew_late(c)
    for c in both:
        for k in corner[c]:
            k.arrived()
        renew_late(c)

    for c in range(chunks):
        for r in rims[c]:
            r.arrived()

    def early(i, _):
        per = 4
        x, y0 = i // (NY // per), i % (NY // per) * per
        g = x * NY // slots
        j0 = x * NY % slots + y0
        ends_all = [
            jnp.where(
                lane % SLOT < SLOT // 2,
                jnp.where(above["gz"], rim_up[c, g], 0.0), jnp.where(below["gz"], rim_low[c, g], 0.0),
            )
            for c in range(chunks)
        ]
        for y1 in range(0, per, 2):
            sides = []
            for y2 in range(2):
                y = y0 + y1 + y2
                z_at = {o: [] for o in range(-H, H + 1) if o}
                for c in range(chunks):
                    u = box[x + H, y + H, rows[c]]
                    ends = pltpu.roll(ends_all[c], lax.rem(NZ - SLOT * (j0 + y1 + y2), NZ), 1)
                    for o in range(1, H + 1):
                        z_at[o].append(split16(pltpu.roll(jnp.where(lane < o, ends, u), NZ - o, 1)))
                        z_at[-o].append(split16(pltpu.roll(jnp.where(lane >= NZ - o, ends, u), o, 1)))
                parts = []
                for a, o in BLOCKS:
                    if a == 2:
                        parts += z_at[o]
                    else:
                        dx, dy = (o, 0) if a == 0 else (0, o)
                        parts += [ub[x + H + dx, y + H + dy, c] for c in range(chunks)]
                sides.append(jnp.concatenate(parts, axis=0))
            out = jnp.dot(s["w_early"][...], jnp.concatenate(sides, axis=1), preferred_element_type=f32)
            for y2 in range(2):
                part = out[:, y2 * NZ:(y2 + 1) * NZ]
                acc[x, y0 + y1 + y2, pl.ds(0, F)] = part[:F] + part[F:2 * F]
                acc[x, y0 + y1 + y2, pl.ds(F, F)] = part[2 * F:]
        return 0

    lax.fori_loop(0, cells // 4, early, 0)

    def late(n):
        a, sign = SIDES[n]
        length = (NX, NY)[a]
        across = (NY, NX)[a]

        def step(p, _):
            sides = []
            for q in range(2):
                parts = []
                for h in range(1, H + 1):
                    at = H + (length - 1 + h if sign > 0 else -h)
                    for c in range(chunks):
                        where = (at, H + 2 * p + q) if a == 0 else (H + 2 * p + q, at)
                        parts.append(split16(box[(*where, rows[c])]))
                sides.append(jnp.concatenate(parts, axis=0))
            out = jnp.dot(s["w_late"][n], jnp.concatenate(sides, axis=1), preferred_element_type=f32)
            for q in range(2):
                part = out[:, q * NZ:(q + 1) * NZ]
                for d in range(H):
                    at = length - 1 - d if sign > 0 else d
                    where = (at, 2 * p + q) if a == 0 else (2 * p + q, at)
                    if d < 2:
                        own_part = part[3 * F * d:3 * F * (d + 1)]
                        acc[(*where, pl.ds(0, F))] += own_part[:F] + own_part[F:2 * F]
                        acc[(*where, pl.ds(F, F))] += own_part[2 * F:]
                    else:
                        acc[(*where, pl.ds(F, F))] += part[6 * F:]
            return 0

        lax.fori_loop(0, across // 2, step, 0)

    for sign in (-1, 1):
        for a in range(2):
            n = SIDES.index((a, sign))
            for m in inside[SIDES[n]]:
                m.arrived()
            pl.when((above if sign > 0 else below)[AXES[a]])(functools.partial(late, n))

    def finish(x, _):
        for y in range(NY):
            u = box[x + H, y + H]
            lapse = (1.0 + 0.25 * jnp.tanh(u[0:1])) * (1.0 / 12.0)
            slope = lapse * acc[x, y, pl.ds(0, F)] + acc[x, y, pl.ds(F, F)] * (1.0 / 64.0)
            slope_ref[x * NY + y] = slope
            value_ref[x * NY + y] = u + 0.125 * slope
        return 0

    lax.fori_loop(0, NX, finish, 0)

    for m in everything:
        m.sent()


def put_out(slope_in, value_in, slope_hbm, value_hbm, sem):
    cells = slope_in.shape[0]

    def step(k, _):
        pltpu.make_async_copy(slope_in.at[k], slope_hbm.at[:, k], sem.at[0]).start()
        pltpu.make_async_copy(value_in.at[k], value_hbm.at[:, k], sem.at[1]).start()
        return 0

    lax.fori_loop(0, cells, step, 0, unroll=8)
    pltpu.make_async_copy(slope_in, value_in, sem.at[0]).wait()
    pltpu.make_async_copy(slope_in, value_in, sem.at[1]).wait()


def local(fields_now, parent, advect, diffuse, box_shift):
    dims = fields_now.shape
    F, NX, NY, NZ = dims
    flat = (F, NX * NY, NZ)
    by_cell = (NX * NY, F, NZ)
    vmem = pl.BlockSpec(memory_space=pltpu.VMEM)
    hbm = pl.BlockSpec(memory_space=pltpu.HBM)
    operands = [
        pltpu.with_memory_space_constraint(x, pltpu.HBM)
        for x in (box_shift, fields_now.reshape(flat), parent.reshape(flat), advect, diffuse, jnp.asarray(coefficients(F)))
    ]
    results = pl.pallas_call(
        functools.partial(kernel, dims),
        out_shape=[pltpu.VMEM(by_cell, f32)] * 2,
        in_specs=[hbm] * 6,
        out_specs=[vmem] * 2,
        scratch_shapes=list(scratch(dims).values()),
        compiler_params=pltpu.CompilerParams(
            collective_id=0, has_side_effects=True, vmem_limit_bytes=VMEM_BYTES
        ),
    )(*operands)
    slope, value = pl.pallas_call(
        put_out,
        out_shape=[jax.ShapeDtypeStruct(flat, f32)] * 2,
        in_specs=[vmem] * 2,
        out_specs=[hbm] * 2,
        scratch_shapes=[pltpu.SemaphoreType.DMA((2,))],
        compiler_params=pltpu.CompilerParams(vmem_limit_bytes=VMEM_BYTES),
    )(*results)
    return slope.reshape(dims), value.reshape(dims)


VMEM_BYTES = 40 * 2**20


def solution(mesh):
    return jax.shard_map(
        local,
        mesh=mesh,
        in_specs=(P(None, "gx", "gy", "gz"), P(None, "gx", "gy", "gz"), P(), P(), P()),
        out_specs=(P(None, "gx", "gy", "gz"), P(None, "gx", "gy", "gz")),
        check_vma=False,
    )
```

time: 38.3 us -> 31.1 us (0.81)
  the two profiles are of different devices: /device:TPU:0 before, /device:TPU:1 now
where the time goes in v1:
time: 31.1 us; the launch traced here: 30.9 us
  Pallas kernels  30.3 us (97%)
  between operations  0.64 us (2%)
    pallas_call x1, Pallas kernels, local(): pl.pallas_call(functools.partial(kernel, dims), out_shape=[pltpu.VMEM(by_...  29.2 us
    pallas_call x1, Pallas kernels, local(): pl.pallas_call(put_out, out_shape=[jax.ShapeDtypeStruct(flat, f32)] * 2,...  1.09 us

profile of v1, /device:TPU:1, one launch (start us, length us, event | category | flops | bytes accessed | tf_op | source)
XLA Modules:
  0.0 30.9 jit_solution(1994862886933106679)
XLA Ops:
  0.6 29.2 %shard_map.77 = (f32[64,24,128]{2,1,0:T(8,128)S(1)}, f32[64,24,128]{2,1,0:T(8,128)S(1)}) custom-call(s32[3]{0:T(128)} %shift_hbm.1, f32[24,64,128]{2,1,0:T(8,128)} %bitcast.4, f32[24,64,128]{2,1,0:T(8,128)} %bitcast.5, f32[3,24,24]{2,1,0:T(8,128)} %advect_hbm.1, f32[3,24,24]{2,1,0:T(8,128)} %diffuse_hbm.1, f32[16,4096]{1,0:T(8,128)} %constant.2.clone.coef_hbm), custom_call_target="tpu_custom_call" | custom-call | tf_op jit(solution)/shard_map/pallas_call | solution.py:644
  29.8 1.1 %shard_map.78 = (f32[24,64,128]{2,1,0:T(8,128)}, f32[24,64,128]{2,1,0:T(8,128)}) custom-call(f32[64,24,128]{2,1,0:T(8,128)S(1)} %get-tuple-element.6.slope_in, f32[64,24,128]{2,1,0:T(8,128)S(1)} %get-tuple-element.7.value_in), custom_call_target="tpu_custom_call" | custom-call | tf_op jit(solution)/shard_map/pallas_call | solution.py:654

commit v2 on v1

--- a/solution.py
+++ b/solution.py
@@ -15,11 +15,13 @@
 ROWS = 8
 AXES = ("gx", "gy", "gz")
 KINDS = ("x", "y", "xy")
-MESSAGES = {"x": 12, "y": 12, "xy": 15}
+ARRIVALS = {"x": 5, "y": 5, "xy": 7}
+ROUTES = 8
 FIRST = {-2: 1, -1: -8, 1: 8, 2: -1}
 SECOND = {-2: -1, -1: 16, 0: -30, 1: 16, 2: -1}
 SIXTH = {-3: 1, -2: -6, -1: 15, 0: -20, 1: 15, 2: -6, 3: 1}
-BLOCKS = [(None, 0)] + [(a, o) for a in range(3) for o in (-3, -2, -1, 1, 2, 3)]
+BLOCKS = [(None, 0)] + [(a, o) for a in range(2) for o in (-3, -2, -1, 1, 2, 3)]
+ALONG = [(2, "first"), (2, "second")]
 SIDES = [(a, sign) for a in range(2) for sign in (-1, 1)]
 f32, bf16 = jnp.float32, jnp.bfloat16
 
@@ -39,6 +41,9 @@
     if block is None:
         return cols
     axis, o = block
+    if o in ("first", "second"):
+        cols[axis + (3 if o == "second" else 0)] = 1
+        return cols
     for a in range(3):
         if axis is None or a == axis:
             cols[a] = FIRST.get(o, 0)
@@ -48,7 +53,7 @@
 
 
 def coefficients(fields):
-    groups = [BLOCKS]
+    groups = [BLOCKS, ALONG]
     for a, sign in SIDES:
         near = [(a, sign * o) for o in range(1, H + 1)]
         groups += [near[d:] + [None] * d for d in range(H)]
@@ -72,6 +77,7 @@
         diffuse=pltpu.VMEM((3, F, F), f32),
         coef=pltpu.VMEM(coefficients(F).shape, f32),
         w_early=pltpu.VMEM((3 * F, len(BLOCKS) * 2 * F), bf16),
+        w_along=pltpu.VMEM((2 * F, len(ALONG) * 2 * F), bf16),
         w_late=pltpu.VMEM((len(SIDES), 7 * F, H * 2 * F), bf16),
         box=pltpu.VMEM((NX + 2 * H, NY + 2 * H, F, NZ), f32),
         ub=pltpu.VMEM((NX + 2 * H, NY + 2 * H, chunks, 2 * ROWS, NZ), bf16),
@@ -96,8 +102,9 @@
             size = (NX, W) if kind == "x" else (W, NY)
             out[f"fw{c}"] = pltpu.VMEM(size + tile, f32)
             out[f"te{c}"] = pltpu.VMEM(size + tile, f32)
-    n = sum(MESSAGES[KINDS[c % 3]] for c in range(chunks))
-    out["send_sem"] = pltpu.SemaphoreType.DMA((n,))
+    out["count"] = pltpu.VMEM((chunks * 8 * NX * NY,) + tile, f32)
+    n = sum(ARRIVALS[KINDS[c % 3]] for c in range(chunks)) + len(SIDES) + 2
+    out["send_sem"] = pltpu.SemaphoreType.DMA((ROUTES,))
     out["recv_sem"] = pltpu.SemaphoreType.DMA((n,))
     out["load_sem"] = pltpu.SemaphoreType.DMA((6,))
     return out
@@ -122,15 +129,13 @@
     kinds = [KINDS[c % 3] for c in range(chunks)]
     rows = [pl.ds(c * ROWS, ROWS) for c in range(chunks)]
 
-    def load_cell(src, dst, n, k):
-        return pltpu.make_async_copy(src.at[:, k], dst.at[k // NY, k % NY], s["load_sem"].at[n])
-
     def load_cells(src, dst, n):
-        def step(k, _):
-            load_cell(src, dst, n, k).start()
+        def step(x, _):
+            for y in range(NY):
+                pltpu.make_async_copy(src.at[:, x * NY + y], dst.at[x, y], s["load_sem"].at[n]).start()
             return 0
 
-        lax.fori_loop(0, cells, step, 0, unroll=8)
+        lax.fori_loop(0, NX, step, 0)
 
     singles = [
         pltpu.make_async_copy(src, dst, s["load_sem"].at[2 + n])
@@ -139,16 +144,35 @@
             (diffuse_hbm, s["diffuse"]), (coef_hbm, s["coef"]),
         ))
     ]
+    DX, DY, DZ = {"gx": -1}, {"gy": -1}, {"gz": -1}
+    UX, UY, UZ = {"gx": 1}, {"gy": 1}, {"gz": 1}
+    barrier = pltpu.get_barrier_semaphore()
+    count = 0
+    for to in (DX, UX, DY, UY, DZ, UZ, UX | UZ, UY | UZ):
+        cond = back = None
+        for a, by in to.items():
+            one, two = (below[a], above[a]) if by < 0 else (above[a], below[a])
+            cond = one if cond is None else cond & one
+            back = two if back is None else back & two
+
+        @pl.when(cond)
+        def _(to=to):
+            pl.semaphore_signal(
+                barrier, inc=1, device_id={a: me[a] + by for a, by in to.items()}, device_id_type=MESH
+            )
+        count = count + jnp.where(back, 1, 0)
+
     singles[0].start()
     load_cells(now_hbm, own, 0)
-
-    class Copy:
-        def __init__(self, src, dst, to, parts=None):
-            n = next(sems)
+    pl.semaphore_wait(barrier, count)
+
+    routes = {}
+
+    class Route:
+        def __init__(self, to):
             self.to = to
-            self.sem = dict(send_sem=s["send_sem"].at[n], recv_sem=s["recv_sem"].at[n])
-            self.parts = parts
-            self.copy = self.make(src, dst)
+            self.send_sem = s["send_sem"].at[len(routes)]
+            self.tiles = 0
             self.sends = self.gets = None
             for a, by in to.items():
                 sends = below[a] if by < 0 else above[a]
@@ -156,51 +180,77 @@
                 self.sends = sends if self.sends is None else self.sends & sends
                 self.gets = gets if self.gets is None else self.gets & gets
 
-        def make(self, src, dst):
+        def copy(self, src, dst, recv_sem):
             return pltpu.make_async_remote_copy(
-                src_ref=src, dst_ref=dst, device_id={a: me[a] + by for a, by in self.to.items()},
-                device_id_type=MESH, **self.sem,
+                src_ref=src, dst_ref=dst, send_sem=self.send_sem, recv_sem=recv_sem,
+                device_id={a: me[a] + by for a, by in self.to.items()}, device_id_type=MESH,
             )
 
+        def all_sent(self):
+            done = s["count"].at[pl.ds(0, self.tiles)]
+            pl.when(self.sends)(self.copy(done, done, s["recv_sem"].at[0]).wait_send)
+
+    def route(to):
+        key = tuple(sorted(to.items()))
+        if key not in routes:
+            routes[key] = Route(to)
+        return routes[key]
+
+    class Arrival:
+        def __init__(self, to):
+            self.route = route(to)
+            self.recv_sem = s["recv_sem"].at[next(sems)]
+            self.tiles = 0
+
+        def arrived(self):
+            done = s["count"].at[pl.ds(0, self.tiles)]
+            pl.when(self.route.gets)(self.route.copy(done, done, self.recv_sem).wait_recv)
+
+    def size_of(ref):
+        return int(np.prod(ref.shape)) // (ROWS * NZ)
+
+    class Message:
+        def __init__(self, src, dst, to, arrival=None, parts=None):
+            self.arrival = arrival or Arrival(to)
+            self.route = route(to)
+            tiles = size_of(dst)
+            self.arrival.tiles += tiles
+            self.route.tiles += tiles
+            self.src, self.dst, self.parts = src, dst, parts
+
         def start(self):
-            pl.when(self.sends)(self.copy.start)
-
-        def start_part(self, i):
-            pl.when(self.sends)(self.make(*self.parts(i)).start)
+            pl.when(self.route.sends)(self.route.copy(self.src, self.dst, self.arrival.recv_sem).start)
+
+        def start_parts(self, i):
+            @pl.when(self.route.sends)
+            def _():
+                for j in range(W):
+                    self.route.copy(*self.parts(i, j), self.arrival.recv_sem).start()
 
         def arrived(self):
-            pl.when(self.gets)(self.copy.wait_recv)
-
-        def sent(self):
-            pl.when(self.sends)(self.copy.wait_send)
-
-    everything = []
-
-    def message(src, dst, to, parts=None):
-        everything.append(Copy(src, dst, to, parts))
-        return everything[-1]
-
-    DX, DY, DZ = {"gx": -1}, {"gy": -1}, {"gz": -1}
-    UX, UY, UZ = {"gx": 1}, {"gy": 1}, {"gz": 1}
+            self.arrival.arrived()
+
+    message = Message
+
     lowx, lowy = pl.ds(0, W), pl.ds(0, W)
     raw, edge, diag, forward, corner = {}, {}, {}, {}, {}
     for c, kind in enumerate(kinds):
         if kind == "x":
-            def cell(i, half, c=c):
-                x, y = i // W, i % W + half * (NY // 2)
+            def cell(i, j, half, c=c):
+                x, y = i, j + half * (NY // 2)
                 return now_hbm.at[rows[c], x * NY + y], s[f"rawx{c}"].at[x, y]
 
             halves = [s[f"rawx{c}"].at[:, pl.ds(h * (NY // 2), NY // 2)] for h in range(2)]
-            raw[c] = [message(r, r, DX, functools.partial(cell, half=h)) for h, r in enumerate(halves)]
+            raw[c] = [message(r, r, DX, parts=functools.partial(cell, half=h)) for h, r in enumerate(halves)]
             diag[c] = [message(epk.at[c, 0], ein.at[c, 2], DX | DZ)]
             forward[c] = message(s[f"fw{c}"], s[f"te{c}"], DY)
         elif kind == "y":
-            def cell(i, half, c=c):
-                x, y = i // W + half * (NX // 2), i % W
+            def cell(i, j, half, c=c):
+                x, y = i + half * (NX // 2), j
                 return now_hbm.at[rows[c], x * NY + y], s[f"rawy{c}"].at[x, y]
 
             halves = [s[f"rawy{c}"].at[pl.ds(h * (NX // 2), NX // 2)] for h in range(2)]
-            raw[c] = [message(r, r, DY, functools.partial(cell, half=h)) for h, r in enumerate(halves)]
+            raw[c] = [message(r, r, DY, parts=functools.partial(cell, half=h)) for h, r in enumerate(halves)]
             diag[c] = [message(epk.at[c, 0], ein.at[c, 2], DY | DZ)]
             forward[c] = message(s[f"fw{c}"], s[f"te{c}"], DX)
         else:
@@ -219,7 +269,8 @@
             ]
         edge[c] = message(epk.at[c, pl.ds(0, 2)], ein.at[c, pl.ds(0, 2)], DZ)
 
-    inside = {side: [] for side in SIDES}
+    inside = {(a, sign): Arrival({AXES[a]: -sign}) for a, sign in SIDES}
+    rims_in = [Arrival(DZ), Arrival(UZ)]
 
     def halo(c, a, by, lo, hi):
         n = (NX, NY)[a]
@@ -228,11 +279,8 @@
         span = pl.ds(H + lo, hi - lo)
         to = {AXES[a]: by}
         if a == 0:
-            m = message(box.at[src, span, rows[c]], box.at[dst, span, rows[c]], to)
-        else:
-            m = message(box.at[span, src, rows[c]], box.at[span, dst, rows[c]], to)
-        inside[(a, -by)].append(m)
-        return m
+            return message(box.at[src, span, rows[c]], box.at[dst, span, rows[c]], to, inside[(a, -by)])
+        return message(box.at[span, src, rows[c]], box.at[span, dst, rows[c]], to, inside[(a, -by)])
 
     early_halo, late_halo, rims = {}, {}, {}
     hx, hy = NX // 2, NY // 2
@@ -246,37 +294,18 @@
         else:
             early_halo[c] = [halo(c, 0, -1, 0, NY), halo(c, 1, -1, 0, NX), halo(c, 0, 1, 0, hy), halo(c, 1, 1, 0, hx)]
             late_halo[c] = [halo(c, 0, 1, hy, NY), halo(c, 1, 1, hx, NX)]
-        rims[c] = [message(rim.at[c], rim_up.at[c], DZ), message(rim.at[c], rim_low.at[c], UZ)]
-
-    barrier = pltpu.get_barrier_semaphore()
-    count = 0
-    for to in (DX, UX, DY, UY, DZ, UZ, UX | UZ, UY | UZ):
-        cond = back = None
-        for a, by in to.items():
-            one, two = (below[a], above[a]) if by < 0 else (above[a], below[a])
-            cond = one if cond is None else cond & one
-            back = two if back is None else back & two
-
-        @pl.when(cond)
-        def _(to=to):
-            pl.semaphore_signal(
-                barrier, inc=1, device_id={a: me[a] + by for a, by in to.items()}, device_id_type=MESH
-            )
-        count = count + jnp.where(back, 1, 0)
-
-    load_cells(parent_hbm, par, 1)
-    for load in singles[1:]:
-        load.start()
-    pl.semaphore_wait(barrier, count)
+        rims[c] = [
+            message(rim.at[c], rim_up.at[c], DZ, rims_in[0]), message(rim.at[c], rim_low.at[c], UZ, rims_in[1]),
+        ]
 
     def send_raw(i, _, half):
         for c, kind in enumerate(kinds):
             if kind != "xy":
-                raw[c][half].start_part(i)
+                raw[c][half].start_parts(i)
         return 0
 
     for half in range(2):
-        lax.fori_loop(0, W * W, functools.partial(send_raw, half=half), 0, unroll=4)
+        lax.fori_loop(0, W, functools.partial(send_raw, half=half), 0)
 
     lane = lax.broadcasted_iota(jnp.int32, (ROWS, NZ), 1)
     thin = lane // W
@@ -308,11 +337,12 @@
             for r in raw[c]:
                 r.start()
 
+    for load in singles[1:]:
+        load.start()
+    load_cells(parent_hbm, par, 1)
     zero16 = jnp.zeros((2 * ROWS, NZ), bf16)
 
     def clear(i, _):
-        for o in (*range(H), *range(H)):
-            pass
         for c in range(chunks):
             for o in range(H):
                 ub[o, i + H, c] = zero16
@@ -361,6 +391,9 @@
             n = min(256, k_early - at)
             s["w_early"][:, at:at + n] = columns(at, 256, range(6))[:, :n].astype(bf16)
         at = up_to(k_early, 256)
+        k_along = len(ALONG) * 2 * F
+        s["w_along"][...] = columns(at, up_to(k_along, 256), (2, 5))[:2 * F, :k_along].astype(bf16)
+        at += up_to(k_along, 256)
         k_late = H * 2 * F
         step = up_to(k_late, 256)
         for n, (a, sign) in enumerate(SIDES):
@@ -520,49 +553,59 @@
             k.arrived()
         renew_late(c)
 
-    for c in range(chunks):
-        for r in rims[c]:
-            r.arrived()
-
-    def early(i, _):
-        per = 4
-        x, y0 = i // (NY // per), i % (NY // per) * per
-        g = x * NY // slots
-        j0 = x * NY % slots + y0
+    def early(x, _):
+        for y0 in range(0, NY, 2):
+            sides = []
+            for y in (y0, y0 + 1):
+                parts = []
+                for a, o in BLOCKS:
+                    dx, dy = (0, o) if a == 1 else (o, 0)
+                    parts += [ub[x + H + dx, y + H + dy, c] for c in range(chunks)]
+                sides.append(jnp.concatenate(parts, axis=0))
+            out = jnp.dot(s["w_early"][...], jnp.concatenate(sides, axis=1), preferred_element_type=f32)
+            for q in range(2):
+                part = out[:, q * NZ:(q + 1) * NZ]
+                acc[x, y0 + q, pl.ds(0, F)] = part[:F] + part[F:2 * F]
+                acc[x, y0 + q, pl.ds(F, F)] = part[2 * F:]
+        return 0
+
+    lax.fori_loop(0, NX, early, 0)
+
+    for r in rims_in:
+        r.arrived()
+
+    def along(x, _):
         ends_all = [
             jnp.where(
                 lane % SLOT < SLOT // 2,
-                jnp.where(above["gz"], rim_up[c, g], 0.0), jnp.where(below["gz"], rim_low[c, g], 0.0),
+                jnp.where(above["gz"], rim_up[c, x * NY // slots], 0.0),
+                jnp.where(below["gz"], rim_low[c, x * NY // slots], 0.0),
             )
             for c in range(chunks)
         ]
-        for y1 in range(0, per, 2):
+        for y0 in range(0, NY, 2):
             sides = []
-            for y2 in range(2):
-                y = y0 + y1 + y2
-                z_at = {o: [] for o in range(-H, H + 1) if o}
+            for y in (y0, y0 + 1):
+                firsts, seconds = [], []
                 for c in range(chunks):
                     u = box[x + H, y + H, rows[c]]
-                    ends = pltpu.roll(ends_all[c], lax.rem(NZ - SLOT * (j0 + y1 + y2), NZ), 1)
+                    ends = pltpu.roll(ends_all[c], lax.rem(2 * NZ - SLOT * (x * NY % slots + y), NZ), 1)
+                    d, t = {}, {}
                     for o in range(1, H + 1):
-                        z_at[o].append(split16(pltpu.roll(jnp.where(lane < o, ends, u), NZ - o, 1)))
-                        z_at[-o].append(split16(pltpu.roll(jnp.where(lane >= NZ - o, ends, u), o, 1)))
-                parts = []
-                for a, o in BLOCKS:
-                    if a == 2:
-                        parts += z_at[o]
-                    else:
-                        dx, dy = (o, 0) if a == 0 else (0, o)
-                        parts += [ub[x + H + dx, y + H + dy, c] for c in range(chunks)]
-                sides.append(jnp.concatenate(parts, axis=0))
-            out = jnp.dot(s["w_early"][...], jnp.concatenate(sides, axis=1), preferred_element_type=f32)
-            for y2 in range(2):
-                part = out[:, y2 * NZ:(y2 + 1) * NZ]
-                acc[x, y0 + y1 + y2, pl.ds(0, F)] = part[:F] + part[F:2 * F]
-                acc[x, y0 + y1 + y2, pl.ds(F, F)] = part[2 * F:]
+                        after = pltpu.roll(jnp.where(lane < o, ends, u), NZ - o, 1)
+                        before = pltpu.roll(jnp.where(lane >= NZ - o, ends, u), o, 1)
+                        d[o], t[o] = after - before, after + before
+                    firsts.append(split16(8.0 * d[1] - d[2]))
+                    seconds.append(split16(16.0 * t[1] - t[2]))
+                    acc[x, y, pl.ds(F + c * ROWS, ROWS)] += t[3] - 6.0 * t[2] + 15.0 * t[1]
+                sides.append(jnp.concatenate(firsts + seconds, axis=0))
+            out = jnp.dot(s["w_along"][...], jnp.concatenate(sides, axis=1), preferred_element_type=f32)
+            for q in range(2):
+                part = out[:, q * NZ:(q + 1) * NZ]
+                acc[x, y0 + q, pl.ds(0, F)] += part[:F] + part[F:]
         return 0
 
-    lax.fori_loop(0, cells // 4, early, 0)
+    lax.fori_loop(0, NX, along, 0)
 
     def late(n):
         a, sign = SIDES[n]
@@ -598,8 +641,7 @@
     for sign in (-1, 1):
         for a in range(2):
             n = SIDES.index((a, sign))
-            for m in inside[SIDES[n]]:
-                m.arrived()
+            inside[SIDES[n]].arrived()
             pl.when((above if sign > 0 else below)[AXES[a]])(functools.partial(late, n))
 
     def finish(x, _):
@@ -613,8 +655,8 @@
 
     lax.fori_loop(0, NX, finish, 0)
 
-    for m in everything:
-        m.sent()
+    for r in routes.values():
+        r.all_sent()
 
 
 def put_out(slope_in, value_in, slope_hbm, value_hbm, sem):

time: 31.1 us -> 26.7 us (0.86)
  the two profiles are of different devices: /device:TPU:1 before, /device:TPU:0 now
where the time goes in v2:
time: 26.7 us; the launch traced here: 26.5 us
  Pallas kernels  25.9 us (97%)
  between operations  0.64 us (2%)
    pallas_call x1, Pallas kernels, local(): pl.pallas_call(functools.partial(kernel, dims), out_shape=[pltpu.VMEM(by_...  24.8 us
    pallas_call x1, Pallas kernels, local(): pl.pallas_call(put_out, out_shape=[jax.ShapeDtypeStruct(flat, f32)] * 2,...  1.09 us

profile of v2, /device:TPU:0, one launch (start us, length us, event | category | flops | bytes accessed | tf_op | source)
XLA Modules:
  0.0 26.5 jit_solution(10155533306783009539)
XLA Ops:
  0.6 24.8 %shard_map.77 = (f32[64,24,128]{2,1,0:T(8,128)S(1)}, f32[64,24,128]{2,1,0:T(8,128)S(1)}) custom-call(s32[3]{0:T(128)} %shift_hbm.1, f32[24,64,128]{2,1,0:T(8,128)} %bitcast.4, f32[24,64,128]{2,1,0:T(8,128)} %bitcast.5, f32[3,24,24]{2,1,0:T(8,128)} %advect_hbm.1, f32[3,24,24]{2,1,0:T(8,128)} %diffuse_hbm.1, f32[16,4096]{1,0:T(8,128)} %constant.2.clone.coef_hbm), custom_call_target="tpu_custom_call" | custom-call | tf_op jit(solution)/shard_map/pallas_call | solution.py:686
  25.4 1.1 %shard_map.78 = (f32[24,64,128]{2,1,0:T(8,128)}, f32[24,64,128]{2,1,0:T(8,128)}) custom-call(f32[64,24,128]{2,1,0:T(8,128)S(1)} %get-tuple-element.6.slope_in, f32[64,24,128]{2,1,0:T(8,128)S(1)} %get-tuple-element.7.value_in), custom_call_target="tpu_custom_call" | custom-call | tf_op jit(solution)/shard_map/pallas_call | solution.py:696

commit v3 on v2

--- a/solution.py
+++ b/solution.py
@@ -55,8 +55,7 @@
 def coefficients(fields):
     groups = [BLOCKS, ALONG]
     for a, sign in SIDES:
-        near = [(a, sign * o) for o in range(1, H + 1)]
-        groups += [near[d:] + [None] * d for d in range(H)]
+        groups += [[(a, sign), (a, 2 * sign)], [(a, 2 * sign), None]]
     out = []
     for g in groups:
         cols = np.concatenate([block_columns(b, fields) for b in g], axis=1)
@@ -78,10 +77,7 @@
         coef=pltpu.VMEM(coefficients(F).shape, f32),
         w_early=pltpu.VMEM((3 * F, len(BLOCKS) * 2 * F), bf16),
         w_along=pltpu.VMEM((2 * F, len(ALONG) * 2 * F), bf16),
-        w_late=pltpu.VMEM((len(SIDES), 7 * F, H * 2 * F), bf16),
-        box=pltpu.VMEM((NX + 2 * H, NY + 2 * H, F, NZ), f32),
         ub=pltpu.VMEM((NX + 2 * H, NY + 2 * H, chunks, 2 * ROWS, NZ), bf16),
-        acc=pltpu.VMEM((NX, NY, 2 * F, NZ), f32),
         rim=pltpu.VMEM((chunks, groups) + tile, f32),
         rim_up=pltpu.VMEM((chunks, groups) + tile, f32),
         rim_low=pltpu.VMEM((chunks, groups) + tile, f32),
@@ -110,14 +106,62 @@
     return out
 
 
+def split16(u):
+    low = u - u.astype(bf16).astype(f32)
+    return jnp.concatenate([u, low], axis=0).astype(bf16)
+
+
+def add_side(box, acc, out_acc, w_late, n, again=None):
+    a, sign = SIDES[n]
+    NX, NY, F, NZ = acc.shape[0], acc.shape[1], acc.shape[2] // 2, acc.shape[3]
+    length, across = ((NX, NY), (NY, NX))[a]
+    linear_rows, smooth_rows = pl.ds(0, F), pl.ds(F, F)
+
+    def spot(depth, i):
+        at = length - 1 - depth if sign > 0 else depth
+        return (at, i) if a == 0 else (i, at)
+
+    for i0 in range(0, across, 2):
+        columns, smooth = [], []
+        for i in (i0, i0 + 1):
+            near = []
+            for h in range(1, H + 1):
+                x, y = spot(-h, i)
+                near.append(box[x + H, y + H])
+            smooth.append((15.0 * near[0] - 6.0 * near[1] + near[2], near[1] - 6.0 * near[0], near[0]))
+            parts = [split16(u[c:c + ROWS]) for u in near[:2] for c in range(0, F, ROWS)]
+            columns.append(jnp.concatenate(parts, axis=0))
+        out = jnp.dot(w_late[n], jnp.concatenate(columns, axis=1), preferred_element_type=f32)
+        for q in range(2):
+            part = out[:, q * NZ:(q + 1) * NZ]
+            for d in range(H):
+                x, y = spot(d, i0 + q)
+                source = out_acc if again is not None and again(x, y) else acc
+                linear = source[x, y, linear_rows]
+                if d < 2:
+                    mine = part[2 * F * d:2 * F * (d + 1)]
+                    linear = linear + (mine[:F] + mine[F:])
+                out_acc[x, y, linear_rows] = linear
+                out_acc[x, y, smooth_rows] = source[x, y, smooth_rows] + smooth[q][d]
+
+
+def finished(box, acc, x, y):
+    u = box[x + H, y + H]
+    F = u.shape[0]
+    lapse = (1.0 + 0.25 * jnp.tanh(u[0:1])) * (1.0 / 12.0)
+    slope = lapse * acc[x, y, pl.ds(0, F)] + acc[x, y, pl.ds(F, F)] * (1.0 / 64.0)
+    return slope, u + 0.125 * slope
+
+
 def kernel(
-    dims, shift_hbm, now_hbm, parent_hbm, advect_hbm, diffuse_hbm, coef_hbm, slope_ref, value_ref, *refs
+    dims, shift_hbm, now_hbm, parent_hbm, advect_hbm, diffuse_hbm, coef_hbm,
+    slope_ref, value_ref, acc, box, w_late, *refs
 ):
     F, NX, NY, NZ = dims
     chunks = F // ROWS
     cells = NX * NY
     s = dict(zip(scratch(dims), refs))
-    own, par, box, ub, acc = s["own"], s["par"], s["box"], s["ub"], s["acc"]
+    own, par, ub = s["own"], s["par"], s["ub"]
     epk, ein, rim, rim_up, rim_low = s["epk"], s["ein"], s["rim"], s["rim_up"], s["rim_low"]
     slots = NZ // SLOT
     groups = cells // slots
@@ -358,10 +402,6 @@
     move = [s["shift"][d] for d in range(3)]
     sz = move[2]
 
-    def split16(u):
-        low = u - u.astype(bf16).astype(f32)
-        return jnp.concatenate([u, low], axis=0).astype(bf16)
-
     def weights():
         mats = []
         for m in (s["advect"], s["diffuse"]):
@@ -375,8 +415,6 @@
             table = s["coef"][:, at:at + width]
             hit = lax.broadcasted_iota(jnp.int32, (F, width), 0).astype(f32) == table[7:8]
             smooth = jnp.where(hit, table[6:7], 0.0)
-            if not ks:
-                return smooth
             total = None
             for k in ks:
                 spread = jnp.where(hit, table[k:k + 1], 0.0).astype(bf16)
@@ -394,12 +432,12 @@
         k_along = len(ALONG) * 2 * F
         s["w_along"][...] = columns(at, up_to(k_along, 256), (2, 5))[:2 * F, :k_along].astype(bf16)
         at += up_to(k_along, 256)
-        k_late = H * 2 * F
+        k_late = 2 * 2 * F
         step = up_to(k_late, 256)
         for n, (a, sign) in enumerate(SIDES):
-            parts = [columns(at + d * step, step, (a, 3 + a) if d < 2 else ()) for d in range(H)]
-            s["w_late"][n] = jnp.concatenate(parts, axis=0)[:, :k_late].astype(bf16)
-            at += H * step
+            parts = [columns(at + d * step, step, (a, 3 + a))[:2 * F] for d in range(2)]
+            w_late[n] = jnp.concatenate(parts, axis=0)[:, :k_late].astype(bf16)
+            at += 2 * step
 
     weights()
 
@@ -569,7 +607,7 @@
                 acc[x, y0 + q, pl.ds(F, F)] = part[2 * F:]
         return 0
 
-    lax.fori_loop(0, NX, early, 0)
+    lax.fori_loop(0, NX, early, 0, unroll=2)
 
     for r in rims_in:
         r.arrived()
@@ -605,71 +643,76 @@
                 acc[x, y0 + q, pl.ds(0, F)] += part[:F] + part[F:]
         return 0
 
-    lax.fori_loop(0, NX, along, 0)
-
-    def late(n):
-        a, sign = SIDES[n]
-        length = (NX, NY)[a]
-        across = (NY, NX)[a]
-
-        def step(p, _):
-            sides = []
-            for q in range(2):
-                parts = []
-                for h in range(1, H + 1):
-                    at = H + (length - 1 + h if sign > 0 else -h)
-                    for c in range(chunks):
-                        where = (at, H + 2 * p + q) if a == 0 else (H + 2 * p + q, at)
-                        parts.append(split16(box[(*where, rows[c])]))
-                sides.append(jnp.concatenate(parts, axis=0))
-            out = jnp.dot(s["w_late"][n], jnp.concatenate(sides, axis=1), preferred_element_type=f32)
-            for q in range(2):
-                part = out[:, q * NZ:(q + 1) * NZ]
-                for d in range(H):
-                    at = length - 1 - d if sign > 0 else d
-                    where = (at, 2 * p + q) if a == 0 else (2 * p + q, at)
-                    if d < 2:
-                        own_part = part[3 * F * d:3 * F * (d + 1)]
-                        acc[(*where, pl.ds(0, F))] += own_part[:F] + own_part[F:2 * F]
-                        acc[(*where, pl.ds(F, F))] += own_part[2 * F:]
-                    else:
-                        acc[(*where, pl.ds(F, F))] += part[6 * F:]
-            return 0
-
-        lax.fori_loop(0, across // 2, step, 0)
-
-    for sign in (-1, 1):
-        for a in range(2):
-            n = SIDES.index((a, sign))
-            inside[SIDES[n]].arrived()
-            pl.when((above if sign > 0 else below)[AXES[a]])(functools.partial(late, n))
+    lax.fori_loop(0, NX, along, 0, unroll=2)
+
+    for a in range(2):
+        n = SIDES.index((a, -1))
+        inside[(a, -1)].arrived()
+        pl.when(below[AXES[a]])(functools.partial(add_side, box, acc, acc, w_late, n))
 
     def finish(x, _):
-        for y in range(NY):
-            u = box[x + H, y + H]
-            lapse = (1.0 + 0.25 * jnp.tanh(u[0:1])) * (1.0 / 12.0)
-            slope = lapse * acc[x, y, pl.ds(0, F)] + acc[x, y, pl.ds(F, F)] * (1.0 / 64.0)
-            slope_ref[x * NY + y] = slope
-            value_ref[x * NY + y] = u + 0.125 * slope
+        for y in range(NY - H):
+            slope_ref[x * NY + y], value_ref[x * NY + y] = finished(box, acc, x, y)
         return 0
 
-    lax.fori_loop(0, NX, finish, 0)
+    lax.fori_loop(0, NX - H, finish, 0)
+
+    for a in range(2):
+        inside[(a, 1)].arrived()
+
+        @pl.when(jnp.logical_not(above[AXES[a]]))
+        def _(a=a):
+            def step(i, _):
+                for h in range(H):
+                    at = (NX, NY)[a] + H + h
+                    where = (at, i + H) if a == 0 else (i + H, at)
+                    box[where] = jnp.zeros((F, NZ), f32)
+                return 0
+
+            lax.fori_loop(0, (NY, NX)[a], step, 0)
 
     for r in routes.values():
         r.all_sent()
 
 
-def put_out(slope_in, value_in, slope_hbm, value_hbm, sem):
-    cells = slope_in.shape[0]
-
-    def step(k, _):
-        pltpu.make_async_copy(slope_in.at[k], slope_hbm.at[:, k], sem.at[0]).start()
-        pltpu.make_async_copy(value_in.at[k], value_hbm.at[:, k], sem.at[1]).start()
+def put_out(slope_in, value_in, acc_in, box, w_late, slope_hbm, value_hbm, slope_rest, value_rest, acc, sem):
+    NX, NY = acc_in.shape[:2]
+    sources = ((slope_in, slope_rest, slope_hbm), (value_in, value_rest, value_hbm))
+
+    def send(x, y, rest):
+        k = x * NY + y
+        for n, source in enumerate(sources):
+            pltpu.make_async_copy(source[rest].at[k], source[2].at[:, k], sem.at[n]).start()
+
+    def send_inner(x, _):
+        for y in range(NY - H):
+            send(x, y, 0)
         return 0
 
-    lax.fori_loop(0, cells, step, 0, unroll=8)
-    pltpu.make_async_copy(slope_in, value_in, sem.at[0]).wait()
-    pltpu.make_async_copy(slope_in, value_in, sem.at[1]).wait()
+    lax.fori_loop(0, NX - H, send_inner, 0)
+    add_side(box, acc_in, acc, w_late, SIDES.index((0, 1)))
+    add_side(box, acc_in, acc, w_late, SIDES.index((1, 1)), lambda x, y: x >= NX - H)
+
+    def finish(x, y):
+        k = x * NY + y
+        slope_rest[k], value_rest[k] = finished(box, acc, x, y)
+
+    def right(x, _):
+        for y in range(NY - H, NY):
+            finish(x, y)
+            send(x, y, 1)
+        return 0
+
+    def low(x, _):
+        for y in range(NY):
+            finish(x, y)
+            send(x, y, 1)
+        return 0
+
+    lax.fori_loop(0, NX - H, right, 0)
+    lax.fori_loop(NX - H, NX, low, 0)
+    for n in range(2):
+        pltpu.make_async_copy(slope_rest, value_rest, sem.at[n]).wait()
 
 
 def local(fields_now, parent, advect, diffuse, box_shift):
@@ -683,11 +726,16 @@
         pltpu.with_memory_space_constraint(x, pltpu.HBM)
         for x in (box_shift, fields_now.reshape(flat), parent.reshape(flat), advect, diffuse, jnp.asarray(coefficients(F)))
     ]
+    held = [
+        pltpu.VMEM((NX, NY, 2 * F, NZ), f32),
+        pltpu.VMEM((NX + 2 * H, NY + 2 * H, F, NZ), f32),
+        pltpu.VMEM((len(SIDES), 4 * F, 4 * F), bf16),
+    ]
     results = pl.pallas_call(
         functools.partial(kernel, dims),
-        out_shape=[pltpu.VMEM(by_cell, f32)] * 2,
+        out_shape=[pltpu.VMEM(by_cell, f32)] * 2 + held,
         in_specs=[hbm] * 6,
-        out_specs=[vmem] * 2,
+        out_specs=[vmem] * 5,
         scratch_shapes=list(scratch(dims).values()),
         compiler_params=pltpu.CompilerParams(
             collective_id=0, has_side_effects=True, vmem_limit_bytes=VMEM_BYTES
@@ -696,9 +744,9 @@
     slope, value = pl.pallas_call(
         put_out,
         out_shape=[jax.ShapeDtypeStruct(flat, f32)] * 2,
-        in_specs=[vmem] * 2,
+        in_specs=[vmem] * 5,
         out_specs=[hbm] * 2,
-        scratch_shapes=[pltpu.SemaphoreType.DMA((2,))],
+        scratch_shapes=[pltpu.VMEM(by_cell, f32)] * 2 + [held[0], pltpu.SemaphoreType.DMA((2,))],
         compiler_params=pltpu.CompilerParams(vmem_limit_bytes=VMEM_BYTES),
     )(*results)
     return slope.reshape(dims), value.reshape(dims)

time: 26.7 us -> 25.4 us (0.951)
  Pallas kernels: 25.9 us -> 24.6 us
    pallas_call x1, Pallas kernels: 24.8 us -> 23.3 us  [local(): pl.pallas_call(functools.partial(kernel, dims), out_shape=[pltpu.VMEM(by_...]
where the time goes in v3:
time: 25.4 us; the launch traced here: 25.2 us
  Pallas kernels  24.6 us (97%)
  between operations  0.64 us (3%)
    pallas_call x1, Pallas kernels, local(): pl.pallas_call(functools.partial(kernel, dims), out_shape=[pltpu.VMEM(by_...  23.3 us
    pallas_call x1, Pallas kernels, local(): pl.pallas_call(put_out, out_shape=[jax.ShapeDtypeStruct(flat, f32)] * 2,...  1.29 us

profile of v3, /device:TPU:0, one launch (start us, length us, event | category | flops | bytes accessed | tf_op | source)
XLA Modules:
  0.0 25.2 jit_solution(2299325653498863153)
XLA Ops:
  0.6 23.3 %shard_map.77 = (f32[64,24,128]{2,1,0:T(8,128)S(1)}, f32[64,24,128]{2,1,0:T(8,128)S(1)}, f32[8,8,48,128]{3,2,1,0:T(8,128)S(1)}, f32[14,14,24,128]{3,2,1,0:T(8,128)S(1)}, bf16[4,96,96]{2,1,0:T(8,128)(2,1)S(1)}) custom-call(s32[3]{0:T(128)} %shift_hbm.1, f32[24,64,128]{2,1,0:T(8,128)} %bitcast.4, f32[24,64,128]{2,1,0:T(8,128)} %bitcast.5, ...), custom_call_target="tpu_custom_call" | custom-call | tf_op jit(solution)/shard_map/pallas_call | solution.py:734
  23.9 1.3 %shard_map.78 = (f32[24,64,128]{2,1,0:T(8,128)}, f32[24,64,128]{2,1,0:T(8,128)}) custom-call(f32[64,24,128]{2,1,0:T(8,128)S(1)} %get-tuple-element.9.slope_in, f32[64,24,128]{2,1,0:T(8,128)S(1)} %get-tuple-element.10.value_in, f32[8,8,48,128]{3,2,1,0:T(8,128)S(1)} %get-tuple-element.11.acc_in, f32[14,14,24,128]{3,2,1,0:T(8,128)S(1)} %get-tuple-element.12.box, ...), custom_call_target="tpu_custom_call" | custom-call | tf_op jit(solution)/shard_map/pallas_call | solution.py:744

commit v4 on v3

--- a/solution.py
+++ b/solution.py
@@ -20,7 +20,7 @@
 FIRST = {-2: 1, -1: -8, 1: 8, 2: -1}
 SECOND = {-2: -1, -1: 16, 0: -30, 1: 16, 2: -1}
 SIXTH = {-3: 1, -2: -6, -1: 15, 0: -20, 1: 15, 2: -6, 3: 1}
-BLOCKS = [(None, 0)] + [(a, o) for a in range(2) for o in (-3, -2, -1, 1, 2, 3)]
+BLOCKS = [(None, 0)] + [(a, o) for a in range(2) for o in (-2, -1, 1, 2)]
 ALONG = [(2, "first"), (2, "second")]
 SIDES = [(a, sign) for a in range(2) for sign in (-1, 1)]
 f32, bf16 = jnp.float32, jnp.bfloat16
@@ -63,6 +63,17 @@
     return np.concatenate(out, axis=1)
 
 
+def band(length):
+    out = np.zeros((2, length, 3, length), np.float32)
+    for n, terms in enumerate((FIRST, SECOND, SIXTH)):
+        for o, factor in terms.items():
+            for lane in range(length):
+                if o:
+                    part, at = divmod(lane + o, length)
+                    out[abs(part), at, n, lane] = factor
+    return out.reshape(2 * length, 3 * length)
+
+
 def scratch(dims):
     F, NX, NY, NZ = dims
     chunks = F // ROWS
@@ -75,6 +86,7 @@
         advect=pltpu.VMEM((3, F, F), f32),
         diffuse=pltpu.VMEM((3, F, F), f32),
         coef=pltpu.VMEM(coefficients(F).shape, f32),
+        band=pltpu.VMEM((2 * NZ, 3 * NZ), bf16),
         w_early=pltpu.VMEM((3 * F, len(BLOCKS) * 2 * F), bf16),
         w_along=pltpu.VMEM((2 * F, len(ALONG) * 2 * F), bf16),
         ub=pltpu.VMEM((NX + 2 * H, NY + 2 * H, chunks, 2 * ROWS, NZ), bf16),
@@ -102,7 +114,7 @@
     n = sum(ARRIVALS[KINDS[c % 3]] for c in range(chunks)) + len(SIDES) + 2
     out["send_sem"] = pltpu.SemaphoreType.DMA((ROUTES,))
     out["recv_sem"] = pltpu.SemaphoreType.DMA((n,))
-    out["load_sem"] = pltpu.SemaphoreType.DMA((6,))
+    out["load_sem"] = pltpu.SemaphoreType.DMA((7,))
     return out
 
 
@@ -154,7 +166,7 @@
 
 
 def kernel(
-    dims, shift_hbm, now_hbm, parent_hbm, advect_hbm, diffuse_hbm, coef_hbm,
+    dims, shift_hbm, now_hbm, parent_hbm, advect_hbm, diffuse_hbm, coef_hbm, band_hbm,
     slope_ref, value_ref, acc, box, w_late, *refs
 ):
     F, NX, NY, NZ = dims
@@ -185,7 +197,7 @@
         pltpu.make_async_copy(src, dst, s["load_sem"].at[2 + n])
         for n, (src, dst) in enumerate((
             (shift_hbm, s["shift"]), (advect_hbm, s["advect"]),
-            (diffuse_hbm, s["diffuse"]), (coef_hbm, s["coef"]),
+            (diffuse_hbm, s["diffuse"]), (coef_hbm, s["coef"]), (band_hbm, s["band"]),
         ))
     ]
     DX, DY, DZ = {"gx": -1}, {"gy": -1}, {"gz": -1}
@@ -348,8 +360,11 @@
                 raw[c][half].start_parts(i)
         return 0
 
-    for half in range(2):
-        lax.fori_loop(0, W, functools.partial(send_raw, half=half), 0)
+    def send_raws(half, lo, hi):
+        lax.fori_loop(lo, hi, functools.partial(send_raw, half=half), 0)
+
+    send_raws(0, 0, W)
+    send_raws(1, 0, W // 2)
 
     lane = lax.broadcasted_iota(jnp.int32, (ROWS, NZ), 1)
     thin = lane // W
@@ -357,29 +372,33 @@
     blank = jnp.zeros((ROWS, NZ), f32)
 
     def pack(c, n, along, q):
-        def step(i, packed):
-            for j in range(NY if along == "x" else NX):
-                x, y = (q * W + i, j) if along == "x" else (j, q * W + i)
-                slot = i * (NY if along == "x" else NX) + j
-                packed = jnp.where(thin == slot, pltpu.roll(own[x, y, rows[c]], W * slot, 1), packed)
-            return packed
-
-        epk[c, n] = lax.fori_loop(0, W, step, blank)
+        packed = blank
+        across = NY if along == "x" else NX
+        for slot in range(W * across):
+            i, j = q * W + slot // across, slot % across
+            x, y = (i, j) if along == "x" else (j, i)
+            packed = jnp.where(thin == slot, pltpu.roll(own[x, y, rows[c]], W * slot, 1), packed)
+        epk[c, n] = packed
 
     pltpu.make_async_copy(par, own, s["load_sem"].at[0]).wait()
-    for c, kind in enumerate(kinds):
-        along = kind[0]
-        for q in range(2):
-            pack(c, q, along, q)
-        if kind == "xy":
-            pack(c, 2, "y", 0)
+    one_way = [c for c in range(chunks) if kinds[c] != "xy"]
+    both = [c for c in range(chunks) if kinds[c] == "xy"]
+    for c in one_way:
+        pack(c, 0, kinds[c], 0)
+        diag[c][0].start()
+    send_raws(1, W // 2, W)
+    for c in one_way:
+        pack(c, 1, kinds[c], 1)
+        edge[c].start()
+    for c in both:
+        pack(c, 0, "x", 0)
+        pack(c, 2, "y", 0)
         for d in diag[c]:
             d.start()
+        for r in raw[c]:
+            r.start()
+        pack(c, 1, "x", 1)
         edge[c].start()
-    for c, kind in enumerate(kinds):
-        if kind == "xy":
-            for r in raw[c]:
-                r.start()
 
     for load in singles[1:]:
         load.start()
@@ -397,12 +416,13 @@
 
     lax.fori_loop(0, NX, clear, 0)
 
-    for load in singles:
-        load.wait()
+    singles[0].wait()
     move = [s["shift"][d] for d in range(3)]
     sz = move[2]
 
     def weights():
+        for load in singles[1:]:
+            load.wait()
         mats = []
         for m in (s["advect"], s["diffuse"]):
             for a in range(3):
@@ -439,40 +459,27 @@
             w_late[n] = jnp.concatenate(parts, axis=0)[:, :k_late].astype(bf16)
             at += 2 * step
 
-    weights()
-
     def z_row(row, packed, slot):
-        tail = pltpu.roll(packed, lax.rem(2 * NZ - W * slot - sz, NZ), 1)
+        tail = pltpu.roll(packed, NZ - W * slot - sz, 1)
         return jnp.where(lane >= NZ - sz, tail, pltpu.roll(row, NZ - sz, 1))
 
-    def z_own(c):
+    def z_own(c, xs, ys):
         kind = kinds[c]
-
-        def step(x, _):
-            for y in range(NY):
+        for x in range(*xs):
+            for y in range(*ys):
                 q, slot = (x // W, x % W * NY + y) if "x" in kind else (y // W, y % W * NX + x)
                 s[f"zs{c}"][x, y] = z_row(own[x, y, rows[c]], ein[c, q], slot)
-            return 0
-
-        lax.fori_loop(0, NX, step, 0)
 
     def z_ext_x(c, lo, hi):
-        def step(x, _):
+        for x in range(W):
             for y in range(lo, hi):
                 s[f"zs{c}"][NX + x, y] = z_row(s[f"rawx{c}"][x, y], ein[c, 2], x * NY + y)
-            return 0
-
-        lax.fori_loop(0, W, step, 0)
 
     def z_ext_y(c, lo, hi):
         n = 3 if kinds[c] == "xy" else 2
-
-        def step(x, _):
+        for x in range(lo, hi):
             for y in range(W):
                 s[f"zs{c}"][x, NY + y] = z_row(s[f"rawy{c}"][x, y], ein[c, n], y * NX + x)
-            return 0
-
-        lax.fori_loop(lo, hi, step, 0)
 
     def make_forward(c):
         zs, fw = s[f"zs{c}"], s[f"fw{c}"]
@@ -536,23 +543,18 @@
         for h in late_halo[c]:
             h.start()
 
-        def step(g, _):
+        for g in range(groups):
             packed = blank
             for j in range(slots):
                 x, y = g * (slots // NY) + j // NY, j % NY
                 packed = jnp.where(wide == j, pltpu.roll(box[x + H, y + H, rows[c]], SLOT * j, 1), packed)
             rim[c, g] = packed
-            return 0
-
-        lax.fori_loop(0, groups, step, 0)
         for r in rims[c]:
             r.start()
 
-    one_way = [c for c in range(chunks) if kinds[c] != "xy"]
-    both = [c for c in range(chunks) if kinds[c] == "xy"]
     for c in one_way:
         edge[c].arrived()
-        z_own(c)
+        z_own(c, (0, NX if kinds[c] == "x" else hx), (0, NY if kinds[c] == "y" else hy))
     for c in one_way:
         diag[c][0].arrived()
         raw[c][0].arrived()
@@ -562,9 +564,11 @@
             z_ext_y(c, 0, hx)
         make_forward(c)
         forward[c].start()
+    for c in one_way:
+        z_own(c, (0 if kinds[c] == "x" else hx, NX), (0 if kinds[c] == "y" else hy, NY))
     for c in both:
         edge[c].arrived()
-        z_own(c)
+        z_own(c, (0, NX), (0, NY))
     for c in one_way:
         raw[c][1].arrived()
         if kinds[c] == "x":
@@ -583,6 +587,7 @@
     pltpu.make_async_copy(own, par, s["load_sem"].at[1]).wait()
     for c in (*one_way, *both):
         renew_early(c)
+    weights()
     for c in one_way:
         forward[c].arrived()
         renew_late(c)
@@ -591,7 +596,7 @@
             k.arrived()
         renew_late(c)
 
-    def early(x, _):
+    def early(x):
         for y0 in range(0, NY, 2):
             sides = []
             for y in (y0, y0 + 1):
@@ -603,47 +608,56 @@
             out = jnp.dot(s["w_early"][...], jnp.concatenate(sides, axis=1), preferred_element_type=f32)
             for q in range(2):
                 part = out[:, q * NZ:(q + 1) * NZ]
+                smooth = part[2 * F:]
+                for o in (-H, H):
+                    for u, v in ((x + o, y0 + q), (x, y0 + q + o)):
+                        if 0 <= u < NX and 0 <= v < NY:
+                            smooth = smooth + box[u + H, v + H]
                 acc[x, y0 + q, pl.ds(0, F)] = part[:F] + part[F:2 * F]
-                acc[x, y0 + q, pl.ds(F, F)] = part[2 * F:]
-        return 0
-
-    lax.fori_loop(0, NX, early, 0, unroll=2)
+                acc[x, y0 + q, pl.ds(F, F)] = smooth
+
+    for x in range(NX):
+        early(x)
 
     for r in rims_in:
         r.arrived()
 
-    def along(x, _):
+    def along(g, _):
         ends_all = [
             jnp.where(
                 lane % SLOT < SLOT // 2,
-                jnp.where(above["gz"], rim_up[c, x * NY // slots], 0.0),
-                jnp.where(below["gz"], rim_low[c, x * NY // slots], 0.0),
+                jnp.where(above["gz"], rim_up[c, g], 0.0), jnp.where(below["gz"], rim_low[c, g], 0.0),
             )
             for c in range(chunks)
         ]
-        for y0 in range(0, NY, 2):
-            sides = []
-            for y in (y0, y0 + 1):
-                firsts, seconds = [], []
+        per = slots // NY
+        for i in range(per):
+            x = g * per + i
+            lines = []
+            for y in range(NY):
                 for c in range(chunks):
-                    u = box[x + H, y + H, rows[c]]
-                    ends = pltpu.roll(ends_all[c], lax.rem(2 * NZ - SLOT * (x * NY % slots + y), NZ), 1)
-                    d, t = {}, {}
-                    for o in range(1, H + 1):
-                        after = pltpu.roll(jnp.where(lane < o, ends, u), NZ - o, 1)
-                        before = pltpu.roll(jnp.where(lane >= NZ - o, ends, u), o, 1)
-                        d[o], t[o] = after - before, after + before
-                    firsts.append(split16(8.0 * d[1] - d[2]))
-                    seconds.append(split16(16.0 * t[1] - t[2]))
-                    acc[x, y, pl.ds(F + c * ROWS, ROWS)] += t[3] - 6.0 * t[2] + 15.0 * t[1]
-                sides.append(jnp.concatenate(firsts + seconds, axis=0))
-            out = jnp.dot(s["w_along"][...], jnp.concatenate(sides, axis=1), preferred_element_type=f32)
-            for q in range(2):
-                part = out[:, q * NZ:(q + 1) * NZ]
-                acc[x, y0 + q, pl.ds(0, F)] += part[:F] + part[F:]
+                    ends = pltpu.roll(ends_all[c], (NZ - SLOT * (i * NY + y)) % NZ, 1)
+                    lines.append(jnp.concatenate([ub[x + H, y + H, c], split16(ends)], axis=1))
+            spread = jnp.dot(jnp.concatenate(lines, axis=0), s["band"][...], preferred_element_type=f32)
+            terms = [
+                spread[n * 2 * ROWS:n * 2 * ROWS + ROWS] + spread[n * 2 * ROWS + ROWS:(n + 1) * 2 * ROWS]
+                for n in range(NY * chunks)
+            ]
+            for y0 in range(0, NY, 2):
+                sides = []
+                for y in (y0, y0 + 1):
+                    mine = terms[y * chunks:(y + 1) * chunks]
+                    parts = [split16(t[:, n * NZ:(n + 1) * NZ]) for n in range(2) for t in mine]
+                    sides.append(jnp.concatenate(parts, axis=0))
+                    for c in range(chunks):
+                        acc[x, y, pl.ds(F + c * ROWS, ROWS)] += mine[c][:, 2 * NZ:]
+                out = jnp.dot(s["w_along"][...], jnp.concatenate(sides, axis=1), preferred_element_type=f32)
+                for q in range(2):
+                    part = out[:, q * NZ:(q + 1) * NZ]
+                    acc[x, y0 + q, pl.ds(0, F)] += part[:F] + part[F:]
         return 0
 
-    lax.fori_loop(0, NX, along, 0, unroll=2)
+    lax.fori_loop(0, groups, along, 0, unroll=4)
 
     for a in range(2):
         n = SIDES.index((a, -1))
@@ -724,7 +738,10 @@
     hbm = pl.BlockSpec(memory_space=pltpu.HBM)
     operands = [
         pltpu.with_memory_space_constraint(x, pltpu.HBM)
-        for x in (box_shift, fields_now.reshape(flat), parent.reshape(flat), advect, diffuse, jnp.asarray(coefficients(F)))
+        for x in (
+            box_shift, fields_now.reshape(flat), parent.reshape(flat), advect, diffuse,
+            jnp.asarray(coefficients(F)), jnp.asarray(band(NZ), bf16),
+        )
     ]
     held = [
         pltpu.VMEM((NX, NY, 2 * F, NZ), f32),
@@ -734,7 +751,7 @@
     results = pl.pallas_call(
         functools.partial(kernel, dims),
         out_shape=[pltpu.VMEM(by_cell, f32)] * 2 + held,
-        in_specs=[hbm] * 6,
+        in_specs=[hbm] * len(operands),
         out_specs=[vmem] * 5,
         scratch_shapes=list(scratch(dims).values()),
         compiler_params=pltpu.CompilerParams(

time: 25.4 us -> 24.1 us (0.949); the launches traced: 25.2 us -> 23.6 us
  Pallas kernels: 24.6 us -> 23 us
    pallas_call x1, Pallas kernels: 23.3 us -> 21.7 us  [local(): pl.pallas_call(functools.partial(kernel, dims), out_shape=[pltpu.VMEM(by_...]
where the time goes in v4:
time: 24.1 us; the launch traced here: 23.6 us
  Pallas kernels  23 us (95%)
  between operations  0.64 us (3%)
    pallas_call x1, Pallas kernels, local(): pl.pallas_call(functools.partial(kernel, dims), out_shape=[pltpu.VMEM(by_...  21.7 us
    pallas_call x1, Pallas kernels, local(): pl.pallas_call(put_out, out_shape=[jax.ShapeDtypeStruct(flat, f32)] * 2,...  1.28 us

profile of v4, /device:TPU:0, one launch (start us, length us, event | category | flops | bytes accessed | tf_op | source)
XLA Modules:
  0.0 23.6 jit_solution(11147716638142269182)
XLA Ops:
  0.6 21.7 %shard_map.86 = (f32[64,24,128]{2,1,0:T(8,128)S(1)}, f32[64,24,128]{2,1,0:T(8,128)S(1)}, f32[8,8,48,128]{3,2,1,0:T(8,128)S(1)}, f32[14,14,24,128]{3,2,1,0:T(8,128)S(1)}, bf16[4,96,96]{2,1,0:T(8,128)(2,1)S(1)}) custom-call(s32[3]{0:T(128)} %shift_hbm.1, f32[24,64,128]{2,1,0:T(8,128)} %bitcast.4, f32[24,64,128]{2,1,0:T(8,128)} %bitcast.5, ...), custom_call_target="tpu_custom_call" | custom-call | tf_op jit(solution)/shard_map/pallas_call | solution.py:751
  22.3 1.3 %shard_map.87 = (f32[24,64,128]{2,1,0:T(8,128)}, f32[24,64,128]{2,1,0:T(8,128)}) custom-call(f32[64,24,128]{2,1,0:T(8,128)S(1)} %get-tuple-element.9.slope_in, f32[64,24,128]{2,1,0:T(8,128)S(1)} %get-tuple-element.10.value_in, f32[8,8,48,128]{3,2,1,0:T(8,128)S(1)} %get-tuple-element.11.acc_in, f32[14,14,24,128]{3,2,1,0:T(8,128)S(1)} %get-tuple-element.12.box, ...), custom_call_target="tpu_custom_call" | custom-call | tf_op jit(solution)/shard_map/pallas_call | solution.py:761

commit v5 on v4

--- a/solution.py
+++ b/solution.py
@@ -14,8 +14,9 @@
 SLOT = 8
 ROWS = 8
 AXES = ("gx", "gy", "gz")
-KINDS = ("x", "y", "xy")
-ARRIVALS = {"x": 5, "y": 5, "xy": 7}
+KINDS = ("x", "y", "split")
+HALF = ROWS // 2
+ARRIVALS = {"x": 5, "y": 5, "split": 7}
 ROUTES = 8
 FIRST = {-2: 1, -1: -8, 1: 8, 2: -1}
 SECOND = {-2: -1, -1: 16, 0: -30, 1: 16, 2: -1}
@@ -68,9 +69,11 @@
     for n, terms in enumerate((FIRST, SECOND, SIXTH)):
         for o, factor in terms.items():
             for lane in range(length):
-                if o:
-                    part, at = divmod(lane + o, length)
-                    out[abs(part), at, n, lane] = factor
+                if o and 0 <= lane + o < length:
+                    out[0, lane + o, n, lane] = factor
+                at = (lane + SLOT // 2) % SLOT - SLOT // 2
+                if (0 <= at + o < H and at < 0) or (-H <= at + o < 0 <= at):
+                    out[1, (lane + o) % length, n, lane] = factor
     return out.reshape(2 * length, 3 * length)
 
 
@@ -98,18 +101,16 @@
     )
     for c in range(chunks):
         kind = KINDS[c % 3]
-        if "x" in kind:
+        if kind != "y":
             out[f"rawx{c}"] = pltpu.VMEM((W, NY) + tile, f32)
-        if "y" in kind:
+        if kind != "x":
             out[f"rawy{c}"] = pltpu.VMEM((NX, W) + tile, f32)
-        ext = (W if "x" in kind else 0, W if "y" in kind else 0)
+        ext = (W if kind != "y" else 0, W if kind != "x" else 0)
         out[f"zs{c}"] = pltpu.VMEM((NX + ext[0], NY + ext[1]) + tile, f32)
-        if kind == "xy":
-            out[f"ce{c}"] = pltpu.VMEM((W, W) + tile, f32)
-        else:
-            size = (NX, W) if kind == "x" else (W, NY)
-            out[f"fw{c}"] = pltpu.VMEM(size + tile, f32)
-            out[f"te{c}"] = pltpu.VMEM(size + tile, f32)
+        for way, size in (("x", (NX, W)), ("y", (W, NY))):
+            if kind in (way, "split"):
+                out[f"fw{way}{c}"] = pltpu.VMEM(size + tile, f32)
+                out[f"te{way}{c}"] = pltpu.VMEM(size + tile, f32)
     out["count"] = pltpu.VMEM((chunks * 8 * NX * NY,) + tile, f32)
     n = sum(ARRIVALS[KINDS[c % 3]] for c in range(chunks)) + len(SIDES) + 2
     out["send_sem"] = pltpu.SemaphoreType.DMA((ROUTES,))
@@ -243,7 +244,7 @@
             )
 
         def all_sent(self):
-            done = s["count"].at[pl.ds(0, self.tiles)]
+            done = s["count"].at[pl.ds(0, self.tiles // 2)]
             pl.when(self.sends)(self.copy(done, done, s["recv_sem"].at[0]).wait_send)
 
     def route(to):
@@ -259,11 +260,11 @@
             self.tiles = 0
 
         def arrived(self):
-            done = s["count"].at[pl.ds(0, self.tiles)]
+            done = s["count"].at[pl.ds(0, self.tiles // 2)]
             pl.when(self.route.gets)(self.route.copy(done, done, self.recv_sem).wait_recv)
 
     def size_of(ref):
-        return int(np.prod(ref.shape)) // (ROWS * NZ)
+        return int(np.prod(ref.shape)) // (HALF * NZ)
 
     class Message:
         def __init__(self, src, dst, to, arrival=None, parts=None):
@@ -289,7 +290,7 @@
     message = Message
 
     lowx, lowy = pl.ds(0, W), pl.ds(0, W)
-    raw, edge, diag, forward, corner = {}, {}, {}, {}, {}
+    raw, edge, diag, forward = {}, {}, {}, {}
     for c, kind in enumerate(kinds):
         if kind == "x":
             def cell(i, j, half, c=c):
@@ -299,7 +300,7 @@
             halves = [s[f"rawx{c}"].at[:, pl.ds(h * (NY // 2), NY // 2)] for h in range(2)]
             raw[c] = [message(r, r, DX, parts=functools.partial(cell, half=h)) for h, r in enumerate(halves)]
             diag[c] = [message(epk.at[c, 0], ein.at[c, 2], DX | DZ)]
-            forward[c] = message(s[f"fw{c}"], s[f"te{c}"], DY)
+            forward[c] = [message(s[f"fwx{c}"], s[f"tex{c}"], DY)]
         elif kind == "y":
             def cell(i, j, half, c=c):
                 x, y = i + half * (NX // 2), j
@@ -308,35 +309,35 @@
             halves = [s[f"rawy{c}"].at[pl.ds(h * (NX // 2), NX // 2)] for h in range(2)]
             raw[c] = [message(r, r, DY, parts=functools.partial(cell, half=h)) for h, r in enumerate(halves)]
             diag[c] = [message(epk.at[c, 0], ein.at[c, 2], DY | DZ)]
-            forward[c] = message(s[f"fw{c}"], s[f"te{c}"], DX)
+            forward[c] = [message(s[f"fwy{c}"], s[f"tey{c}"], DX)]
         else:
+            a_rows, b_rows = pl.ds(0, HALF), pl.ds(HALF, HALF)
             raw[c] = [
-                message(own.at[lowx, :, rows[c]], s[f"rawx{c}"], DX),
-                message(own.at[:, lowy, rows[c]], s[f"rawy{c}"], DY),
+                message(own.at[lowx, :, pl.ds(c * ROWS, HALF)], s[f"rawx{c}"].at[:, :, a_rows], DX),
+                message(own.at[:, lowy, pl.ds(c * ROWS + HALF, HALF)], s[f"rawy{c}"].at[:, :, b_rows], DY),
             ]
             diag[c] = [
                 message(epk.at[c, 0], ein.at[c, 2], DX | DZ), message(epk.at[c, 2], ein.at[c, 3], DY | DZ),
             ]
-            near, far = pl.ds(0, W // 2), pl.ds(W // 2, W // 2)
-            zs, ce = s[f"zs{c}"], s[f"ce{c}"]
-            corner[c] = [
-                message(zs.at[far, pl.ds(NY, W)], ce.at[far], DX),
-                message(zs.at[pl.ds(NX, W // 2), lowy], ce.at[near], DY),
+            forward[c] = [
+                message(s[f"fwx{c}"].at[:, :, a_rows], s[f"tex{c}"].at[:, :, a_rows], DY),
+                message(s[f"fwy{c}"].at[:, :, b_rows], s[f"tey{c}"].at[:, :, b_rows], DX),
             ]
         edge[c] = message(epk.at[c, pl.ds(0, 2)], ein.at[c, pl.ds(0, 2)], DZ)
 
     inside = {(a, sign): Arrival({AXES[a]: -sign}) for a, sign in SIDES}
     rims_in = [Arrival(DZ), Arrival(UZ)]
 
-    def halo(c, a, by, lo, hi):
+    def halo(c, a, by, lo, hi, part=None):
+        fields = rows[c] if part is None else pl.ds(c * ROWS + part * HALF, HALF)
         n = (NX, NY)[a]
         src = pl.ds(H, H) if by < 0 else pl.ds(n, H)
         dst = pl.ds(n + H, H) if by < 0 else pl.ds(0, H)
         span = pl.ds(H + lo, hi - lo)
         to = {AXES[a]: by}
         if a == 0:
-            return message(box.at[src, span, rows[c]], box.at[dst, span, rows[c]], to, inside[(a, -by)])
-        return message(box.at[span, src, rows[c]], box.at[span, dst, rows[c]], to, inside[(a, -by)])
+            return message(box.at[src, span, fields], box.at[dst, span, fields], to, inside[(a, -by)])
+        return message(box.at[span, src, fields], box.at[span, dst, fields], to, inside[(a, -by)])
 
     early_halo, late_halo, rims = {}, {}, {}
     hx, hy = NX // 2, NY // 2
@@ -348,15 +349,20 @@
             early_halo[c] = [halo(c, 0, -1, 0, NY), halo(c, 1, 1, 0, hx)]
             late_halo[c] = [halo(c, 1, -1, 0, NX), halo(c, 1, 1, hx, NX), halo(c, 0, 1, 0, NY)]
         else:
-            early_halo[c] = [halo(c, 0, -1, 0, NY), halo(c, 1, -1, 0, NX), halo(c, 0, 1, 0, hy), halo(c, 1, 1, 0, hx)]
-            late_halo[c] = [halo(c, 0, 1, hy, NY), halo(c, 1, 1, hx, NX)]
+            early_halo[c] = [
+                halo(c, 1, -1, 0, NX, 0), halo(c, 0, -1, 0, NY, 1), halo(c, 0, 1, 0, hy, 0), halo(c, 1, 1, 0, hx, 1),
+            ]
+            late_halo[c] = [
+                halo(c, 0, -1, 0, NY, 0), halo(c, 1, -1, 0, NX, 1), halo(c, 0, 1, hy, NY, 0),
+                halo(c, 1, 1, hx, NX, 1), halo(c, 0, 1, 0, NY, 1), halo(c, 1, 1, 0, NX, 0),
+            ]
         rims[c] = [
             message(rim.at[c], rim_up.at[c], DZ, rims_in[0]), message(rim.at[c], rim_low.at[c], UZ, rims_in[1]),
         ]
 
     def send_raw(i, _, half):
         for c, kind in enumerate(kinds):
-            if kind != "xy":
+            if kind != "split":
                 raw[c][half].start_parts(i)
         return 0
 
@@ -381,8 +387,8 @@
         epk[c, n] = packed
 
     pltpu.make_async_copy(par, own, s["load_sem"].at[0]).wait()
-    one_way = [c for c in range(chunks) if kinds[c] != "xy"]
-    both = [c for c in range(chunks) if kinds[c] == "xy"]
+    one_way = [c for c in range(chunks) if kinds[c] != "split"]
+    both = [c for c in range(chunks) if kinds[c] == "split"]
     for c in one_way:
         pack(c, 0, kinds[c], 0)
         diag[c][0].start()
@@ -467,7 +473,7 @@
         kind = kinds[c]
         for x in range(*xs):
             for y in range(*ys):
-                q, slot = (x // W, x % W * NY + y) if "x" in kind else (y // W, y % W * NX + x)
+                q, slot = (x // W, x % W * NY + y) if kind != "y" else (y // W, y % W * NX + x)
                 s[f"zs{c}"][x, y] = z_row(own[x, y, rows[c]], ein[c, q], slot)
 
     def z_ext_x(c, lo, hi):
@@ -476,27 +482,31 @@
                 s[f"zs{c}"][NX + x, y] = z_row(s[f"rawx{c}"][x, y], ein[c, 2], x * NY + y)
 
     def z_ext_y(c, lo, hi):
-        n = 3 if kinds[c] == "xy" else 2
+        n = 3 if kinds[c] == "split" else 2
         for x in range(lo, hi):
             for y in range(W):
                 s[f"zs{c}"][x, NY + y] = z_row(s[f"rawy{c}"][x, y], ein[c, n], y * NX + x)
 
     def make_forward(c):
-        zs, fw = s[f"zs{c}"], s[f"fw{c}"]
+        zs = s[f"zs{c}"]
 
         def step(i, _):
             for j in range(W):
-                if kinds[c] == "x":
-                    fw[i, j] = zs[i + move[0], j]
-                else:
-                    fw[j, i] = zs[j, i + move[1]]
+                if kinds[c] != "y":
+                    s[f"fwx{c}"][i, j] = zs[i + move[0], j]
+                if kinds[c] != "x":
+                    s[f"fwy{c}"][j, i] = zs[j, i + move[1]]
             return 0
 
-        lax.fori_loop(0, NX if kinds[c] == "x" else NY, step, 0)
+        lax.fori_loop(0, NX, step, 0)
+        for f in forward[c]:
+            f.start()
 
     in_z = me["gz"] * NZ + lane + sz < size["gz"] * NZ
 
-    def renew(c, xs, ys, late):
+    upper = lax.broadcasted_iota(jnp.int32, (ROWS, NZ), 0) < HALF
+
+    def renew(c, xs, ys, late, part=None, whole=True):
         kind, zs = kinds[c], s[f"zs{c}"]
 
         def step(x, _):
@@ -504,20 +514,28 @@
             for y in range(*ys):
                 in_y = me["gy"] * NY + y + move[1] < size["gy"] * NY
                 X, Y = x + move[0], y + move[1]
-                if not late:
+                if late:
+                    if kind != "y":
+                        x_first = jnp.where(
+                            Y < NY, zs[X, jnp.minimum(Y, NY - 1)], s[f"tex{c}"][x, jnp.maximum(Y - NY, 0)]
+                        )
+                    if kind != "x":
+                        y_first = jnp.where(
+                            X < NX, zs[jnp.minimum(X, NX - 1), Y], s[f"tey{c}"][jnp.maximum(X - NX, 0), y]
+                        )
+                    row = x_first if kind == "x" else y_first
+                    if kind == "split":
+                        row = jnp.where(upper, x_first, y_first)
+                else:
                     row = zs[X, Y]
-                elif kind == "x":
-                    row = jnp.where(Y < NY, zs[X, jnp.minimum(Y, NY - 1)], s[f"te{c}"][x, jnp.maximum(Y - NY, 0)])
-                elif kind == "y":
-                    row = jnp.where(X < NX, zs[jnp.minimum(X, NX - 1), Y], s[f"te{c}"][jnp.maximum(X - NX, 0), y])
+                row = jnp.where(in_z & (in_x & in_y), row, par[x, y, rows[c]])
+                if part is None:
+                    box[x + H, y + H, rows[c]] = row
                 else:
-                    row = jnp.where(
-                        (X < NX) | (Y < NY), zs[X, Y],
-                        s[f"ce{c}"][jnp.maximum(X - NX, 0), jnp.maximum(Y - NY, 0)],
-                    )
-                row = jnp.where(in_z & (in_x & in_y), row, par[x, y, rows[c]])
-                box[x + H, y + H, rows[c]] = row
-                ub[x + H, y + H, c] = split16(row)
+                    kept = slice(part * HALF, (part + 1) * HALF)
+                    box[x + H, y + H, pl.ds(c * ROWS + part * HALF, HALF)] = row[kept]
+                if whole:
+                    ub[x + H, y + H, c] = split16(row)
             return 0
 
         lax.fori_loop(*xs, step, 0)
@@ -528,17 +546,22 @@
         elif kinds[c] == "y":
             renew(c, (0, hx), (0, NY), False)
         else:
-            renew(c, (0, hx), (0, NY), False)
-            renew(c, (hx, NX), (0, hy), False)
+            renew(c, (0, hx), (0, hy), False)
+            renew(c, (hx, NX), (0, hy), False, 0, False)
+            renew(c, (0, hx), (hy, NY), False, 1, False)
         for h in early_halo[c]:
             h.start()
 
     def renew_late(c):
+        for f in forward[c]:
+            f.arrived()
         if kinds[c] == "x":
             renew(c, (0, NX), (hy, NY), True)
         elif kinds[c] == "y":
             renew(c, (hx, NX), (0, NY), True)
         else:
+            renew(c, (hx, NX), (0, hy), True, 1)
+            renew(c, (0, hx), (hy, NY), True, 0)
             renew(c, (hx, NX), (hy, NY), True)
         for h in late_halo[c]:
             h.start()
@@ -563,7 +586,6 @@
         else:
             z_ext_y(c, 0, hx)
         make_forward(c)
-        forward[c].start()
     for c in one_way:
         z_own(c, (0 if kinds[c] == "x" else hx, NX), (0 if kinds[c] == "y" else hy, NY))
     for c in both:
@@ -582,18 +604,12 @@
         z_ext_x(c, 0, NY)
         raw[c][1].arrived()
         z_ext_y(c, 0, NX)
-        for k in corner[c]:
-            k.start()
+        make_forward(c)
     pltpu.make_async_copy(own, par, s["load_sem"].at[1]).wait()
     for c in (*one_way, *both):
         renew_early(c)
     weights()
-    for c in one_way:
-        forward[c].arrived()
-        renew_late(c)
-    for c in both:
-        for k in corner[c]:
-            k.arrived()
+    for c in (*one_way, *both):
         renew_late(c)
 
     def early(x):
@@ -619,45 +635,57 @@
     for x in range(NX):
         early(x)
 
+    def summed(spread, n):
+        at = n * 2 * ROWS
+        return spread[at:at + ROWS] + spread[at + ROWS:at + 2 * ROWS]
+
+    def mixed_along(columns):
+        sides = [
+            jnp.concatenate([split16(t[:, n * NZ:(n + 1) * NZ]) for n in range(2) for t in terms], axis=0)
+            for terms in columns
+        ]
+        out = jnp.dot(s["w_along"][...], jnp.concatenate(sides, axis=1), preferred_element_type=f32)
+        out = out[:F] + out[F:]
+        return [out[:, q * NZ:(q + 1) * NZ] for q in range(2)]
+
+    def along(x):
+        lines = [ub[x + H, y + H, c] for y in range(NY) for c in range(chunks)]
+        spread = jnp.dot(jnp.concatenate(lines, axis=0), s["band"][:NZ], preferred_element_type=f32)
+        terms = [[summed(spread, y * chunks + c) for c in range(chunks)] for y in range(NY)]
+        for y0 in range(0, NY, 2):
+            linear = mixed_along(terms[y0:y0 + 2])
+            for q in range(2):
+                acc[x, y0 + q, pl.ds(0, F)] += linear[q]
+                for c in range(chunks):
+                    acc[x, y0 + q, pl.ds(F + c * ROWS, ROWS)] += terms[y0 + q][c][:, 2 * NZ:]
+
+    for x in range(NX):
+        along(x)
+
     for r in rims_in:
         r.arrived()
 
-    def along(g, _):
-        ends_all = [
-            jnp.where(
+    lines = []
+    for g in range(groups):
+        for c in range(chunks):
+            lines.append(split16(jnp.where(
                 lane % SLOT < SLOT // 2,
                 jnp.where(above["gz"], rim_up[c, g], 0.0), jnp.where(below["gz"], rim_low[c, g], 0.0),
-            )
-            for c in range(chunks)
-        ]
-        per = slots // NY
-        for i in range(per):
-            x = g * per + i
-            lines = []
-            for y in range(NY):
-                for c in range(chunks):
-                    ends = pltpu.roll(ends_all[c], (NZ - SLOT * (i * NY + y)) % NZ, 1)
-                    lines.append(jnp.concatenate([ub[x + H, y + H, c], split16(ends)], axis=1))
-            spread = jnp.dot(jnp.concatenate(lines, axis=0), s["band"][...], preferred_element_type=f32)
-            terms = [
-                spread[n * 2 * ROWS:n * 2 * ROWS + ROWS] + spread[n * 2 * ROWS + ROWS:(n + 1) * 2 * ROWS]
-                for n in range(NY * chunks)
-            ]
-            for y0 in range(0, NY, 2):
-                sides = []
-                for y in (y0, y0 + 1):
-                    mine = terms[y * chunks:(y + 1) * chunks]
-                    parts = [split16(t[:, n * NZ:(n + 1) * NZ]) for n in range(2) for t in mine]
-                    sides.append(jnp.concatenate(parts, axis=0))
-                    for c in range(chunks):
-                        acc[x, y, pl.ds(F + c * ROWS, ROWS)] += mine[c][:, 2 * NZ:]
-                out = jnp.dot(s["w_along"][...], jnp.concatenate(sides, axis=1), preferred_element_type=f32)
-                for q in range(2):
-                    part = out[:, q * NZ:(q + 1) * NZ]
-                    acc[x, y0 + q, pl.ds(0, F)] += part[:F] + part[F:]
-        return 0
-
-    lax.fori_loop(0, groups, along, 0, unroll=4)
+            )))
+    spread = jnp.dot(jnp.concatenate(lines, axis=0), s["band"][NZ:], preferred_element_type=f32)
+    terms = [[summed(spread, g * chunks + c) for c in range(chunks)] for g in range(groups)]
+    at_ends = (lane < SLOT // 2) | (lane >= NZ - SLOT // 2)
+    for g0 in range(0, groups, 2):
+        linear = mixed_along(terms[g0:g0 + 2])
+        for q in range(2):
+            g = g0 + q
+            lapse = (1.0 + 0.25 * jnp.tanh(rim[0, g, 0:1, :])) * (64.0 / 12.0)
+            for c in range(chunks):
+                extra = lapse * linear[q][c * ROWS:(c + 1) * ROWS] + terms[g][c][:, 2 * NZ:]
+                for j in range(slots):
+                    x, y = g * (slots // NY) + j // NY, j % NY
+                    placed = jnp.where(at_ends, pltpu.roll(extra, (NZ - SLOT * j) % NZ, 1), 0.0)
+                    acc[x, y, pl.ds(F + c * ROWS, ROWS)] += placed
 
     for a in range(2):
         n = SIDES.index((a, -1))

time: 24.1 us -> 23.7 us (0.983); the launches traced: 23.6 us -> 23.6 us
  no operation moved by 1% of the time
where the time goes in v5:
time: 23.7 us; the launch traced here: 23.6 us
  Pallas kernels  22.9 us (97%)
  between operations  0.64 us (3%)
    pallas_call x1, Pallas kernels, local(): pl.pallas_call(functools.partial(kernel, dims), out_shape=[pltpu.VMEM(by_...  21.7 us
    pallas_call x1, Pallas kernels, local(): pl.pallas_call(put_out, out_shape=[jax.ShapeDtypeStruct(flat, f32)] * 2,...  1.29 us

profile of v5, /device:TPU:0, one launch (start us, length us, event | category | flops | bytes accessed | tf_op | source)
XLA Modules:
  0.0 23.6 jit_solution(2134408757168543722)
XLA Ops:
  0.6 21.7 %shard_map.86 = (f32[64,24,128]{2,1,0:T(8,128)S(1)}, f32[64,24,128]{2,1,0:T(8,128)S(1)}, f32[8,8,48,128]{3,2,1,0:T(8,128)S(1)}, f32[14,14,24,128]{3,2,1,0:T(8,128)S(1)}, bf16[4,96,96]{2,1,0:T(8,128)(2,1)S(1)}) custom-call(s32[3]{0:T(128)} %shift_hbm.1, f32[24,64,128]{2,1,0:T(8,128)} %bitcast.4, f32[24,64,128]{2,1,0:T(8,128)} %bitcast.5, ...), custom_call_target="tpu_custom_call" | custom-call | tf_op jit(solution)/shard_map/pallas_call | solution.py:779
  22.3 1.3 %shard_map.87 = (f32[24,64,128]{2,1,0:T(8,128)}, f32[24,64,128]{2,1,0:T(8,128)}) custom-call(f32[64,24,128]{2,1,0:T(8,128)S(1)} %get-tuple-element.9.slope_in, f32[64,24,128]{2,1,0:T(8,128)S(1)} %get-tuple-element.10.value_in, f32[8,8,48,128]{3,2,1,0:T(8,128)S(1)} %get-tuple-element.11.acc_in, f32[14,14,24,128]{3,2,1,0:T(8,128)S(1)} %get-tuple-element.12.box, ...), custom_call_target="tpu_custom_call" | custom-call | tf_op jit(solution)/shard_map/pallas_call | solution.py:789

commit v6 on v5

--- a/solution.py
+++ b/solution.py
@@ -291,6 +291,18 @@
 
     lowx, lowy = pl.ds(0, W), pl.ds(0, W)
     raw, edge, diag, forward = {}, {}, {}, {}
+    whole = pl.ds(0, ROWS)
+
+    def halves_of(src, dst, way, fields, to):
+        arrival = Arrival(to)
+        out = []
+        for h in range(2):
+            n = (NX if way == "x" else NY) // 2
+            span = pl.ds(h * n, n)
+            at = (span, slice(None), fields) if way == "x" else (slice(None), span, fields)
+            out.append([message(src.at[at], dst.at[at], to, arrival)])
+        return out
+
     for c, kind in enumerate(kinds):
         if kind == "x":
             def cell(i, j, half, c=c):
@@ -300,7 +312,7 @@
             halves = [s[f"rawx{c}"].at[:, pl.ds(h * (NY // 2), NY // 2)] for h in range(2)]
             raw[c] = [message(r, r, DX, parts=functools.partial(cell, half=h)) for h, r in enumerate(halves)]
             diag[c] = [message(epk.at[c, 0], ein.at[c, 2], DX | DZ)]
-            forward[c] = [message(s[f"fwx{c}"], s[f"tex{c}"], DY)]
+            forward[c] = halves_of(s[f"fwx{c}"], s[f"tex{c}"], "x", whole, DY)
         elif kind == "y":
             def cell(i, j, half, c=c):
                 x, y = i + half * (NX // 2), j
@@ -309,7 +321,7 @@
             halves = [s[f"rawy{c}"].at[pl.ds(h * (NX // 2), NX // 2)] for h in range(2)]
             raw[c] = [message(r, r, DY, parts=functools.partial(cell, half=h)) for h, r in enumerate(halves)]
             diag[c] = [message(epk.at[c, 0], ein.at[c, 2], DY | DZ)]
-            forward[c] = [message(s[f"fwy{c}"], s[f"tey{c}"], DX)]
+            forward[c] = halves_of(s[f"fwy{c}"], s[f"tey{c}"], "y", whole, DX)
         else:
             a_rows, b_rows = pl.ds(0, HALF), pl.ds(HALF, HALF)
             raw[c] = [
@@ -319,10 +331,9 @@
             diag[c] = [
                 message(epk.at[c, 0], ein.at[c, 2], DX | DZ), message(epk.at[c, 2], ein.at[c, 3], DY | DZ),
             ]
-            forward[c] = [
-                message(s[f"fwx{c}"].at[:, :, a_rows], s[f"tex{c}"].at[:, :, a_rows], DY),
-                message(s[f"fwy{c}"].at[:, :, b_rows], s[f"tey{c}"].at[:, :, b_rows], DX),
-            ]
+            along_x = halves_of(s[f"fwx{c}"], s[f"tex{c}"], "x", a_rows, DY)
+            along_y = halves_of(s[f"fwy{c}"], s[f"tey{c}"], "y", b_rows, DX)
+            forward[c] = [x + y for x, y in zip(along_x, along_y)]
         edge[c] = message(epk.at[c, pl.ds(0, 2)], ein.at[c, pl.ds(0, 2)], DZ)
 
     inside = {(a, sign): Arrival({AXES[a]: -sign}) for a, sign in SIDES}
@@ -487,7 +498,7 @@
             for y in range(W):
                 s[f"zs{c}"][x, NY + y] = z_row(s[f"rawy{c}"][x, y], ein[c, n], y * NX + x)
 
-    def make_forward(c):
+    def make_forward(c, half):
         zs = s[f"zs{c}"]
 
         def step(i, _):
@@ -498,8 +509,8 @@
                     s[f"fwy{c}"][j, i] = zs[j, i + move[1]]
             return 0
 
-        lax.fori_loop(0, NX, step, 0)
-        for f in forward[c]:
+        lax.fori_loop(half * hx, (half + 1) * hx, step, 0)
+        for f in forward[c][half]:
             f.start()
 
     in_z = me["gz"] * NZ + lane + sz < size["gz"] * NZ
@@ -553,7 +564,7 @@
             h.start()
 
     def renew_late(c):
-        for f in forward[c]:
+        for f in forward[c][0]:
             f.arrived()
         if kinds[c] == "x":
             renew(c, (0, NX), (hy, NY), True)
@@ -578,6 +589,13 @@
     for c in one_way:
         edge[c].arrived()
         z_own(c, (0, NX if kinds[c] == "x" else hx), (0, NY if kinds[c] == "y" else hy))
+        make_forward(c, 0)
+    for c in both:
+        edge[c].arrived()
+        z_own(c, (0, NX), (0, NY))
+        make_forward(c, 0)
+    for c in one_way:
+        z_own(c, (0 if kinds[c] == "x" else hx, NX), (0 if kinds[c] == "y" else hy, NY))
     for c in one_way:
         diag[c][0].arrived()
         raw[c][0].arrived()
@@ -585,12 +603,7 @@
             z_ext_x(c, 0, hy)
         else:
             z_ext_y(c, 0, hx)
-        make_forward(c)
-    for c in one_way:
-        z_own(c, (0 if kinds[c] == "x" else hx, NX), (0 if kinds[c] == "y" else hy, NY))
-    for c in both:
-        edge[c].arrived()
-        z_own(c, (0, NX), (0, NY))
+        make_forward(c, 1)
     for c in one_way:
         raw[c][1].arrived()
         if kinds[c] == "x":
@@ -604,7 +617,7 @@
         z_ext_x(c, 0, NY)
         raw[c][1].arrived()
         z_ext_y(c, 0, NX)
-        make_forward(c)
+        make_forward(c, 1)
     pltpu.make_async_copy(own, par, s["load_sem"].at[1]).wait()
     for c in (*one_way, *both):
         renew_early(c)

time: 23.7 us -> 23.1 us (0.975)
  Pallas kernels: 22.9 us -> 22.3 us
    pallas_call x1, Pallas kernels: 21.7 us -> 21 us  [local(): pl.pallas_call(functools.partial(kernel, dims), out_shape=[pltpu.VMEM(by_...]
where the time goes in v6:
time: 23.1 us; the launch traced here: 22.9 us
  Pallas kernels  22.3 us (97%)
  between operations  0.64 us (3%)
    pallas_call x1, Pallas kernels, local(): pl.pallas_call(functools.partial(kernel, dims), out_shape=[pltpu.VMEM(by_...  21 us
    pallas_call x1, Pallas kernels, local(): pl.pallas_call(put_out, out_shape=[jax.ShapeDtypeStruct(flat, f32)] * 2,...  1.29 us

profile of v6, /device:TPU:0, one launch (start us, length us, event | category | flops | bytes accessed | tf_op | source)
XLA Modules:
  0.0 22.9 jit_solution(266944089411204919)
XLA Ops:
  0.6 21.0 %shard_map.86 = (f32[64,24,128]{2,1,0:T(8,128)S(1)}, f32[64,24,128]{2,1,0:T(8,128)S(1)}, f32[8,8,48,128]{3,2,1,0:T(8,128)S(1)}, f32[14,14,24,128]{3,2,1,0:T(8,128)S(1)}, bf16[4,96,96]{2,1,0:T(8,128)(2,1)S(1)}) custom-call(s32[3]{0:T(128)} %shift_hbm.1, f32[24,64,128]{2,1,0:T(8,128)} %bitcast.4, f32[24,64,128]{2,1,0:T(8,128)} %bitcast.5, ...), custom_call_target="tpu_custom_call" | custom-call | tf_op jit(solution)/shard_map/pallas_call | solution.py:792
  21.6 1.3 %shard_map.87 = (f32[24,64,128]{2,1,0:T(8,128)}, f32[24,64,128]{2,1,0:T(8,128)}) custom-call(f32[64,24,128]{2,1,0:T(8,128)S(1)} %get-tuple-element.9.slope_in, f32[64,24,128]{2,1,0:T(8,128)S(1)} %get-tuple-element.10.value_in, f32[8,8,48,128]{3,2,1,0:T(8,128)S(1)} %get-tuple-element.11.acc_in, f32[14,14,24,128]{3,2,1,0:T(8,128)S(1)} %get-tuple-element.12.box, ...), custom_call_target="tpu_custom_call" | custom-call | tf_op jit(solution)/shard_map/pallas_call | solution.py:802

commit v7 on v6

--- a/solution.py
+++ b/solution.py
@@ -267,22 +267,16 @@
         return int(np.prod(ref.shape)) // (HALF * NZ)
 
     class Message:
-        def __init__(self, src, dst, to, arrival=None, parts=None):
+        def __init__(self, src, dst, to, arrival=None):
             self.arrival = arrival or Arrival(to)
             self.route = route(to)
             tiles = size_of(dst)
             self.arrival.tiles += tiles
             self.route.tiles += tiles
-            self.src, self.dst, self.parts = src, dst, parts
+            self.src, self.dst = src, dst
 
         def start(self):
             pl.when(self.route.sends)(self.route.copy(self.src, self.dst, self.arrival.recv_sem).start)
-
-        def start_parts(self, i):
-            @pl.when(self.route.sends)
-            def _():
-                for j in range(W):
-                    self.route.copy(*self.parts(i, j), self.arrival.recv_sem).start()
 
         def arrived(self):
             self.arrival.arrived()
@@ -305,21 +299,13 @@
 
     for c, kind in enumerate(kinds):
         if kind == "x":
-            def cell(i, j, half, c=c):
-                x, y = i, j + half * (NY // 2)
-                return now_hbm.at[rows[c], x * NY + y], s[f"rawx{c}"].at[x, y]
-
-            halves = [s[f"rawx{c}"].at[:, pl.ds(h * (NY // 2), NY // 2)] for h in range(2)]
-            raw[c] = [message(r, r, DX, parts=functools.partial(cell, half=h)) for h, r in enumerate(halves)]
+            spans = [pl.ds(h * (NY // 2), NY // 2) for h in range(2)]
+            raw[c] = [message(own.at[lowx, n, rows[c]], s[f"rawx{c}"].at[:, n], DX) for n in spans]
             diag[c] = [message(epk.at[c, 0], ein.at[c, 2], DX | DZ)]
             forward[c] = halves_of(s[f"fwx{c}"], s[f"tex{c}"], "x", whole, DY)
         elif kind == "y":
-            def cell(i, j, half, c=c):
-                x, y = i + half * (NX // 2), j
-                return now_hbm.at[rows[c], x * NY + y], s[f"rawy{c}"].at[x, y]
-
-            halves = [s[f"rawy{c}"].at[pl.ds(h * (NX // 2), NX // 2)] for h in range(2)]
-            raw[c] = [message(r, r, DY, parts=functools.partial(cell, half=h)) for h, r in enumerate(halves)]
+            spans = [pl.ds(h * (NX // 2), NX // 2) for h in range(2)]
+            raw[c] = [message(own.at[n, lowy, rows[c]], s[f"rawy{c}"].at[n], DY) for n in spans]
             diag[c] = [message(epk.at[c, 0], ein.at[c, 2], DY | DZ)]
             forward[c] = halves_of(s[f"fwy{c}"], s[f"tey{c}"], "y", whole, DX)
         else:
@@ -371,18 +357,6 @@
             message(rim.at[c], rim_up.at[c], DZ, rims_in[0]), message(rim.at[c], rim_low.at[c], UZ, rims_in[1]),
         ]
 
-    def send_raw(i, _, half):
-        for c, kind in enumerate(kinds):
-            if kind != "split":
-                raw[c][half].start_parts(i)
-        return 0
-
-    def send_raws(half, lo, hi):
-        lax.fori_loop(lo, hi, functools.partial(send_raw, half=half), 0)
-
-    send_raws(0, 0, W)
-    send_raws(1, 0, W // 2)
-
     lane = lax.broadcasted_iota(jnp.int32, (ROWS, NZ), 1)
     thin = lane // W
     wide = ((lane + SLOT // 2) % NZ) // SLOT
@@ -401,9 +375,11 @@
     one_way = [c for c in range(chunks) if kinds[c] != "split"]
     both = [c for c in range(chunks) if kinds[c] == "split"]
     for c in one_way:
+        raw[c][0].start()
+    for c in one_way:
         pack(c, 0, kinds[c], 0)
         diag[c][0].start()
-    send_raws(1, W // 2, W)
+        raw[c][1].start()
     for c in one_way:
         pack(c, 1, kinds[c], 1)
         edge[c].start()
@@ -739,12 +715,9 @@
         for n, source in enumerate(sources):
             pltpu.make_async_copy(source[rest].at[k], source[2].at[:, k], sem.at[n]).start()
 
-    def send_inner(x, _):
+    for x in range(NX - H):
         for y in range(NY - H):
             send(x, y, 0)
-        return 0
-
-    lax.fori_loop(0, NX - H, send_inner, 0)
     add_side(box, acc_in, acc, w_late, SIDES.index((0, 1)))
     add_side(box, acc_in, acc, w_late, SIDES.index((1, 1)), lambda x, y: x >= NX - H)
 
@@ -752,20 +725,10 @@
         k = x * NY + y
         slope_rest[k], value_rest[k] = finished(box, acc, x, y)
 
-    def right(x, _):
-        for y in range(NY - H, NY):
+    for x in range(NX):
+        for y in range(NY - H if x < NX - H else 0, NY):
             finish(x, y)
             send(x, y, 1)
-        return 0
-
-    def low(x, _):
-        for y in range(NY):
-            finish(x, y)
-            send(x, y, 1)
-        return 0
-
-    lax.fori_loop(0, NX - H, right, 0)
-    lax.fori_loop(NX - H, NX, low, 0)
     for n in range(2):
         pltpu.make_async_copy(slope_rest, value_rest, sem.at[n]).wait()
 

time: 23.1 us -> 22.7 us (0.983)
  Pallas kernels: 22.3 us -> 22 us
where the time goes in v7:
time: 22.7 us; the launch traced here: 22.6 us
  Pallas kernels  22 us (97%)
  between operations  0.64 us (3%)
    pallas_call x1, Pallas kernels, local(): pl.pallas_call(functools.partial(kernel, dims), out_shape=[pltpu.VMEM(by_...  20.8 us
    pallas_call x1, Pallas kernels, local(): pl.pallas_call(put_out, out_shape=[jax.ShapeDtypeStruct(flat, f32)] * 2,...  1.15 us

profile of v7, /device:TPU:0, one launch (start us, length us, event | category | flops | bytes accessed | tf_op | source)
XLA Modules:
  0.0 22.6 jit_solution(3487425042944245810)
XLA Ops:
  0.6 20.8 %shard_map.86 = (f32[64,24,128]{2,1,0:T(8,128)S(1)}, f32[64,24,128]{2,1,0:T(8,128)S(1)}, f32[8,8,48,128]{3,2,1,0:T(8,128)S(1)}, f32[14,14,24,128]{3,2,1,0:T(8,128)S(1)}, bf16[4,96,96]{2,1,0:T(8,128)(2,1)S(1)}) custom-call(s32[3]{0:T(128)} %shift_hbm.1, f32[24,64,128]{2,1,0:T(8,128)} %bitcast.4, f32[24,64,128]{2,1,0:T(8,128)} %bitcast.5, ...), custom_call_target="tpu_custom_call" | custom-call | tf_op jit(solution)/shard_map/pallas_call | solution.py:755
  21.4 1.2 %shard_map.87 = (f32[24,64,128]{2,1,0:T(8,128)}, f32[24,64,128]{2,1,0:T(8,128)}) custom-call(f32[64,24,128]{2,1,0:T(8,128)S(1)} %get-tuple-element.9.slope_in, f32[64,24,128]{2,1,0:T(8,128)S(1)} %get-tuple-element.10.value_in, f32[8,8,48,128]{3,2,1,0:T(8,128)S(1)} %get-tuple-element.11.acc_in, f32[14,14,24,128]{3,2,1,0:T(8,128)S(1)} %get-tuple-element.12.box, ...), custom_call_target="tpu_custom_call" | custom-call | tf_op jit(solution)/shard_map/pallas_call | solution.py:765

commit v8 on v6

--- a/solution.py
+++ b/solution.py
@@ -205,7 +205,7 @@
     UX, UY, UZ = {"gx": 1}, {"gy": 1}, {"gz": 1}
     barrier = pltpu.get_barrier_semaphore()
     count = 0
-    for to in (DX, UX, DY, UY, DZ, UZ, UX | UZ, UY | UZ):
+    for to in (UX, UY, UZ, UX | UZ, UY | UZ):
         cond = back = None
         for a, by in to.items():
             one, two = (below[a], above[a]) if by < 0 else (above[a], below[a])
@@ -221,7 +221,10 @@
 
     singles[0].start()
     load_cells(now_hbm, own, 0)
-    pl.semaphore_wait(barrier, count)
+    @pl.when(count > 0)
+    def _():
+        pl.semaphore_wait(barrier, count)
+
 
     routes = {}
 
@@ -739,12 +742,9 @@
         for n, source in enumerate(sources):
             pltpu.make_async_copy(source[rest].at[k], source[2].at[:, k], sem.at[n]).start()
 
-    def send_inner(x, _):
+    for x in range(NX - H):
         for y in range(NY - H):
             send(x, y, 0)
-        return 0
-
-    lax.fori_loop(0, NX - H, send_inner, 0)
     add_side(box, acc_in, acc, w_late, SIDES.index((0, 1)))
     add_side(box, acc_in, acc, w_late, SIDES.index((1, 1)), lambda x, y: x >= NX - H)
 
@@ -752,20 +752,10 @@
         k = x * NY + y
         slope_rest[k], value_rest[k] = finished(box, acc, x, y)
 
-    def right(x, _):
-        for y in range(NY - H, NY):
+    for x in range(NX):
+        for y in range(NY - H if x < NX - H else 0, NY):
             finish(x, y)
             send(x, y, 1)
-        return 0
-
-    def low(x, _):
-        for y in range(NY):
-            finish(x, y)
-            send(x, y, 1)
-        return 0
-
-    lax.fori_loop(0, NX - H, right, 0)
-    lax.fori_loop(NX - H, NX, low, 0)
     for n in range(2):
         pltpu.make_async_copy(slope_rest, value_rest, sem.at[n]).wait()
 

time: 23.1 us -> 21.8 us (0.944)
  Pallas kernels: 22.3 us -> 21 us
    pallas_call x1, Pallas kernels: 21 us -> 19.9 us  [local(): pl.pallas_call(functools.partial(kernel, dims), out_shape=[pltpu.VMEM(by_...]
where the time goes in v8:
time: 21.8 us; the launch traced here: 21.7 us
  Pallas kernels  21 us (96%)
  between operations  0.64 us (3%)
    pallas_call x1, Pallas kernels, local(): pl.pallas_call(functools.partial(kernel, dims), out_shape=[pltpu.VMEM(by_...  19.9 us
    pallas_call x1, Pallas kernels, local(): pl.pallas_call(put_out, out_shape=[jax.ShapeDtypeStruct(flat, f32)] * 2,...  1.15 us

profile of v8, /device:TPU:0, one launch (start us, length us, event | category | flops | bytes accessed | tf_op | source)
XLA Modules:
  0.0 21.7 jit_solution(8587029188922389637)
XLA Ops:
  0.6 19.9 %shard_map.86 = (f32[64,24,128]{2,1,0:T(8,128)S(1)}, f32[64,24,128]{2,1,0:T(8,128)S(1)}, f32[8,8,48,128]{3,2,1,0:T(8,128)S(1)}, f32[14,14,24,128]{3,2,1,0:T(8,128)S(1)}, bf16[4,96,96]{2,1,0:T(8,128)(2,1)S(1)}) custom-call(s32[3]{0:T(128)} %shift_hbm.1, f32[24,64,128]{2,1,0:T(8,128)} %bitcast.4, f32[24,64,128]{2,1,0:T(8,128)} %bitcast.5, ...), custom_call_target="tpu_custom_call" | custom-call | tf_op jit(solution)/shard_map/pallas_call | solution.py:782
  20.5 1.2 %shard_map.87 = (f32[24,64,128]{2,1,0:T(8,128)}, f32[24,64,128]{2,1,0:T(8,128)}) custom-call(f32[64,24,128]{2,1,0:T(8,128)S(1)} %get-tuple-element.9.slope_in, f32[64,24,128]{2,1,0:T(8,128)S(1)} %get-tuple-element.10.value_in, f32[8,8,48,128]{3,2,1,0:T(8,128)S(1)} %get-tuple-element.11.acc_in, f32[14,14,24,128]{3,2,1,0:T(8,128)S(1)} %get-tuple-element.12.box, ...), custom_call_target="tpu_custom_call" | custom-call | tf_op jit(solution)/shard_map/pallas_call | solution.py:792

commit v9 on v8

--- a/solution.py
+++ b/solution.py
@@ -313,7 +313,10 @@
                 return now_hbm.at[rows[c], x * NY + y], s[f"rawx{c}"].at[x, y]
 
             halves = [s[f"rawx{c}"].at[:, pl.ds(h * (NY // 2), NY // 2)] for h in range(2)]
-            raw[c] = [message(r, r, DX, parts=functools.partial(cell, half=h)) for h, r in enumerate(halves)]
+            raw[c] = [
+                message(halves[0], halves[0], DX, parts=functools.partial(cell, half=0)),
+                message(own.at[lowx, pl.ds(NY // 2, NY // 2), rows[c]], halves[1], DX),
+            ]
             diag[c] = [message(epk.at[c, 0], ein.at[c, 2], DX | DZ)]
             forward[c] = halves_of(s[f"fwx{c}"], s[f"tex{c}"], "x", whole, DY)
         elif kind == "y":
@@ -322,7 +325,10 @@
                 return now_hbm.at[rows[c], x * NY + y], s[f"rawy{c}"].at[x, y]
 
             halves = [s[f"rawy{c}"].at[pl.ds(h * (NX // 2), NX // 2)] for h in range(2)]
-            raw[c] = [message(r, r, DY, parts=functools.partial(cell, half=h)) for h, r in enumerate(halves)]
+            raw[c] = [
+                message(halves[0], halves[0], DY, parts=functools.partial(cell, half=0)),
+                message(own.at[pl.ds(NX // 2, NX // 2), lowy, rows[c]], halves[1], DY),
+            ]
             diag[c] = [message(epk.at[c, 0], ein.at[c, 2], DY | DZ)]
             forward[c] = halves_of(s[f"fwy{c}"], s[f"tey{c}"], "y", whole, DX)
         else:
@@ -384,7 +390,6 @@
         lax.fori_loop(lo, hi, functools.partial(send_raw, half=half), 0)
 
     send_raws(0, 0, W)
-    send_raws(1, 0, W // 2)
 
     lane = lax.broadcasted_iota(jnp.int32, (ROWS, NZ), 1)
     thin = lane // W
@@ -406,7 +411,7 @@
     for c in one_way:
         pack(c, 0, kinds[c], 0)
         diag[c][0].start()
-    send_raws(1, W // 2, W)
+        raw[c][1].start()
     for c in one_way:
         pack(c, 1, kinds[c], 1)
         edge[c].start()

time: 21.8 us -> 21.8 us (level)
  no operation moved by 1% of the time
where the time goes in v9:
time: 21.8 us; the launch traced here: 21.7 us
  Pallas kernels  21 us (96%)
  between operations  0.64 us (3%)
    pallas_call x1, Pallas kernels, local(): pl.pallas_call(functools.partial(kernel, dims), out_shape=[pltpu.VMEM(by_...  19.9 us
    pallas_call x1, Pallas kernels, local(): pl.pallas_call(put_out, out_shape=[jax.ShapeDtypeStruct(flat, f32)] * 2,...  1.15 us

profile of v9, /device:TPU:0, one launch (start us, length us, event | category | flops | bytes accessed | tf_op | source)
XLA Modules:
  0.0 21.7 jit_solution(1320902777886686347)
XLA Ops:
  0.6 19.9 %shard_map.86 = (f32[64,24,128]{2,1,0:T(8,128)S(1)}, f32[64,24,128]{2,1,0:T(8,128)S(1)}, f32[8,8,48,128]{3,2,1,0:T(8,128)S(1)}, f32[14,14,24,128]{3,2,1,0:T(8,128)S(1)}, bf16[4,96,96]{2,1,0:T(8,128)(2,1)S(1)}) custom-call(s32[3]{0:T(128)} %shift_hbm.1, f32[24,64,128]{2,1,0:T(8,128)} %bitcast.4, f32[24,64,128]{2,1,0:T(8,128)} %bitcast.5, ...), custom_call_target="tpu_custom_call" | custom-call | tf_op jit(solution)/shard_map/pallas_call | solution.py:787
  20.5 1.2 %shard_map.87 = (f32[24,64,128]{2,1,0:T(8,128)}, f32[24,64,128]{2,1,0:T(8,128)}) custom-call(f32[64,24,128]{2,1,0:T(8,128)S(1)} %get-tuple-element.9.slope_in, f32[64,24,128]{2,1,0:T(8,128)S(1)} %get-tuple-element.10.value_in, f32[8,8,48,128]{3,2,1,0:T(8,128)S(1)} %get-tuple-element.11.acc_in, f32[14,14,24,128]{3,2,1,0:T(8,128)S(1)} %get-tuple-element.12.box, ...), custom_call_target="tpu_custom_call" | custom-call | tf_op jit(solution)/shard_map/pallas_call | solution.py:797
